TPU v7x, 32 devices: a whole 2x2x4 slice. The times are simulated.
32 devices in a mesh: dp: 8 (over z, y), mp: 4 (over x, core).
Axes of the slice: x: 2, y: 2, z: 4, core: 2. Of those that a mesh axis runs over, the one named last changes fastest.
Arguments:
- inputs: bfloat16 [8192, 768], P(('dp', 'mp')), may hold values from -6 to 6
- memory: bfloat16 [32768, 768], P(('dp', 'mp')), may hold values from -6 to 6
- target_len: int32 [64], P('dp'), may hold values from 8 to 114, as said below
- memory_len: int32 [64], P('dp'), may hold values from 32 to 512, as said below
- bucket_map: int32 [128], replicated, may hold values from 0 to 31, as said below
- self_gain: float32 [768], replicated, may hold values from 0.5 to 1.5
- self_query: bfloat16 [768, 768], P(None, 'mp'), may hold values from -0.02734375 to 0.02734375
- self_key: bfloat16 [768, 768], P(None, 'mp'), may hold values from -0.21875 to 0.21875
- self_value: bfloat16 [768, 768], P(None, 'mp'), may hold values from -0.21875 to 0.21875
- self_out: bfloat16 [768, 768], P('mp'), may hold values from -1.25 to 1.25
- bias_table: float32 [32, 12], P(None, 'mp'), may hold values from -4 to 4
- cross_gain: float32 [768], replicated, may hold values from 0.5 to 1.5
- cross_query: bfloat16 [768, 768], P(None, 'mp'), may hold values from -0.02734375 to 0.02734375
- cross_key: bfloat16 [768, 768], P(None, 'mp'), may hold values from -0.21875 to 0.21875
- cross_value: bfloat16 [768, 768], P(None, 'mp'), may hold values from -0.21875 to 0.21875
- cross_out: bfloat16 [768, 768], P('mp'), may hold values from -2.5 to 2.5
- feed_gain: float32 [768], replicated, may hold values from 0.5 to 1.5
- feed_input: bfloat16 [768, 3072], P(None, 'mp'), may hold values from -0.21875 to 0.21875
- feed_output: bfloat16 [3072, 768], P('mp'), may hold values from -0.15625 to 0.15625
- cotangent: bfloat16 [8192, 768], P(('dp', 'mp')), may hold values from -6 to 6
Outputs:
- layer_out: bfloat16 [8192, 768], P(('dp', 'mp'))
- inputs_grad: float32 [8192, 768], P(('dp', 'mp'))
- memory_grad: float32 [32768, 768], P(('dp', 'mp'))
- self_gain_grad: float32 [768], replicated
- self_query_grad: float32 [768, 768], P(None, 'mp')
- self_key_grad: float32 [768, 768], P(None, 'mp')
- self_value_grad: float32 [768, 768], P(None, 'mp')
- self_out_grad: float32 [768, 768], P('mp')
- bias_table_grad: float32 [32, 12], P(None, 'mp')
- cross_gain_grad: float32 [768], replicated
- cross_query_grad: float32 [768, 768], P(None, 'mp')
- cross_key_grad: float32 [768, 768], P(None, 'mp')
- cross_value_grad: float32 [768, 768], P(None, 'mp')
- cross_out_grad: float32 [768, 768], P('mp')
- feed_gain_grad: float32 [768], replicated
- feed_input_grad: float32 [768, 3072], P(None, 'mp')
- feed_output_grad: float32 [3072, 768], P('mp')
Inputs may be any that keep to these rules, and one draw needn't show every extreme that they name: bucket_map[d] is the bucket of a key d positions before its query: it equals d below 16, never falls as d grows, and reaches 31. An example's target rows at positions from target_len on are padding. An example's memory rows at positions from memory_len on are padding.
All inputs are finite; a program needn't handle non-finite values.
Results may differ from a plain program's by a relative error of at most 0.023.
Values may be sent and summed in bfloat16 or wider, within the bound.
No kernel may reach another device: no remote copies, remote signals or barrier semaphores. Data moves between devices by JAX's collectives and lax.ppermute only.
A program may use at most 128 MiB of HBM per device.

v0:
```python
import functools

import jax
import jax.numpy as jnp
from jax import lax
from jax.experimental import pallas as pl
from jax.experimental.pallas import tpu as pltpu
from jax.sharding import PartitionSpec as P

HEAD_DIM = 64
PAIR = 2 * HEAD_DIM
BUCKETS = 32
TGT_LEN = 128
MEM_LEN = 512

masked_fill = -1000000000.0
epsilon = 1e-06
highest = lax.Precision.HIGHEST
tanh_scale = 0.7978845608
cubic_term = 0.044715
bf16 = jnp.bfloat16
f32 = jnp.float32


def dot_nn(a, b):
    return lax.dot_general(a, b, (((1,), (0,)), ((), ())), preferred_element_type=f32)


def dot_nt(a, b):
    return lax.dot_general(a, b, (((1,), (1,)), ((), ())), preferred_element_type=f32)


def dot_tn(a, b):
    return lax.dot_general(a, b, (((0,), (0,)), ((), ())), preferred_element_type=f32)


def row_scale(hidden):
    return lax.rsqrt(jnp.mean(hidden * hidden, -1, keepdims=True) + epsilon)


def norm_backward(hidden, scale, gain, upstream):
    weighted = gain * upstream
    return scale * weighted - hidden * (scale * scale * scale) * jnp.mean(hidden * weighted, -1, keepdims=True)


def matrix(blocks, index, width):
    return jnp.concatenate([b[index * width : (index + 1) * width, :] for b in blocks], 0)


def store_rows(ref, lead, index, grad, turn):
    blocks = ref.shape[len(lead)]
    size = grad.shape[0] // blocks
    for a in range(blocks):
        ref[(*lead, a ^ turn, slice(index * size, (index + 1) * size))] = grad[a * size : (a + 1) * size].astype(bf16)


def store_extra(ref, lead, start, rows, turn):
    for a in range(ref.shape[len(lead)]):
        ref[(*lead, a ^ turn, slice(start, start + EXTRA))] = (rows if a == 0 else jnp.zeros_like(rows)).astype(bf16)


EXTRA = 8


def first_of(turn_ref):
    return turn_ref[1] == 0


def passed_on(blocks, first, index):
    own, core, far, far_y, both, both_y = blocks
    width = far.shape[0]
    rows = slice(index * width, (index + 1) * width)
    straight = first == (index == 0)
    pieces = [own[rows, :], core[rows, :]]
    for here, there in ((far, far_y), (both, both_y)):
        pieces.append(jnp.where(straight, here[...], there[...]))
    return jnp.concatenate(pieces, 0)


def store_halves(low_ref, high_ref, ref):
    half = ref.shape[0] // 2
    low_ref[...] = ref[:half]
    high_ref[...] = ref[half:]


def store_grad(keep_ref, send_ref, index, grad, turn):
    width = grad.shape[0] // 4
    for j in range(4):
        store_rows((keep_ref, send_ref)[j % 2], (j // 2,), index, grad[j * width : (j + 1) * width], turn)


def pair_masks():
    lane = lax.broadcasted_iota(jnp.int32, (1, PAIR), 1)
    return (lane < HEAD_DIM).astype(bf16), (lane >= HEAD_DIM).astype(bf16)


def stack_pair(rows, masks):
    return jnp.concatenate([rows * masks[0], rows * masks[1]], 0)


def unstack_pair(both):
    lane = lax.broadcasted_iota(jnp.int32, (TGT_LEN, PAIR), 1)
    return jnp.where(lane < HEAD_DIM, both[:TGT_LEN], both[TGT_LEN:])


def softmax_rows(scores):
    weights = jnp.exp(scores - jnp.max(scores, -1, keepdims=True))
    return weights * (1.0 / jnp.sum(weights, -1, keepdims=True))


def locate(step, pairs, keys):
    example = lax.div(step, pairs)
    pair = lax.rem(step, pairs)
    rows = pl.ds(pl.multiple_of(example * TGT_LEN, TGT_LEN), TGT_LEN)
    key_rows = pl.ds(pl.multiple_of(example * keys, keys), keys)
    cols = pl.ds(pl.multiple_of(pair * PAIR, PAIR), PAIR)
    return example, pair, rows, key_rows, cols


def cross_probs(queries, key_rows, length):
    scores = dot_nt(queries, key_rows)
    key = lax.broadcasted_iota(jnp.int32, scores.shape, 1)
    return softmax_rows(jnp.where(key < length, scores, masked_fill))


def attend(q_ref, k_ref, v_ref, mixed_ref, keys, probs_of):
    masks = pair_masks()
    pairs = q_ref.shape[1] // PAIR
    examples = q_ref.shape[0] // TGT_LEN

    def step(i, carry):
        example, pair, rows, key_rows, cols = locate(i, pairs, keys)
        probs = probs_of(stack_pair(q_ref[rows, cols], masks), k_ref[key_rows, cols], example, pair)
        mixed = dot_nn(probs.astype(bf16), v_ref[key_rows, cols])
        mixed_ref[rows, cols] = unstack_pair(mixed).astype(bf16)
        return carry

    lax.fori_loop(0, examples * pairs, step, 0, unroll=2)


def attend_back(q_ref, k_ref, v_ref, m_ref, dq_ref, dk_ref, dv_ref, keys, probs_of):
    masks = pair_masks()
    pairs = q_ref.shape[1] // PAIR
    examples = q_ref.shape[0] // TGT_LEN

    def step(i, carry):
        example, pair, rows, key_rows, cols = locate(i, pairs, keys)
        queries = stack_pair(q_ref[rows, cols], masks)
        grads = stack_pair(m_ref[rows, cols], masks)
        key_block = k_ref[key_rows, cols]
        probs = probs_of(queries, key_block, example, pair)
        dv_ref[cols, key_rows] = dot_tn(grads, probs.astype(bf16)).astype(bf16)
        prob_grad = dot_nt(grads, v_ref[key_rows, cols])
        score_grad = probs * (prob_grad - jnp.sum(probs * prob_grad, -1, keepdims=True))
        low = score_grad.astype(bf16)
        dq_ref[rows, cols] = unstack_pair(dot_nn(low, key_block)).astype(bf16)
        dk_ref[cols, key_rows] = dot_tn(queries, low).astype(bf16)
        return carry

    lax.fori_loop(0, examples * pairs, step, 0, unroll=UNROLL)


UNROLL = 4


def fill_bias(table_ref, bias_ref):
    for head in range(bias_ref.shape[0] // TGT_LEN):
        row = jnp.broadcast_to(table_ref[head : head + 1, :], (TGT_LEN, TGT_LEN))
        bias_ref[head * TGT_LEN : (head + 1) * TGT_LEN, :] = pltpu.roll(row, 0, axis=1, stride=1, stride_axis=0)


def stack_heads(rows):
    lane = lax.broadcasted_iota(jnp.int32, (1, rows.shape[1]), 1)
    heads = rows.shape[1] // HEAD_DIM
    return jnp.concatenate([rows * (lax.div(lane, HEAD_DIM) == h).astype(bf16) for h in range(heads)], 0)


def unstack_heads(stacked):
    length = TGT_LEN
    lane = lax.broadcasted_iota(jnp.int32, (length, stacked.shape[1]), 1)
    out = stacked[:length]
    for h in range(1, stacked.shape[1] // HEAD_DIM):
        out = jnp.where(lane >= h * HEAD_DIM, stacked[h * length : (h + 1) * length], out)
    return out


def self_probs(queries, key_rows, bias, length):
    scores = dot_nt(queries, key_rows) + bias
    key = lax.broadcasted_iota(jnp.int32, scores.shape, 1)
    query = lax.rem(lax.broadcasted_iota(jnp.int32, scores.shape, 0), TGT_LEN)
    return softmax_rows(jnp.where((key <= query) & (key < length), scores, masked_fill))


def diagonal_sums(grad):
    query = lax.broadcasted_iota(jnp.int32, grad.shape, 0)
    for bit in range(TGT_LEN.bit_length() - 1):
        moved = pltpu.roll(grad, TGT_LEN - (1 << bit), axis=1)
        grad = jnp.where((query >> bit) & 1 == 1, moved, grad)
    return jnp.sum(grad, 0, keepdims=True)


def first_norm(x_ref, gain_ref, n_ref):
    hidden = x_ref[...].astype(f32)
    n_ref[...] = (hidden * row_scale(hidden) * gain_ref[...].reshape(1, -1)).astype(bf16)


def self_forward(
    base, n0, n1, wq_ref, wk_ref, wv_ref, wo_ref, table_ref, rank_ref, len_ref,
    q_ref, k_ref, v_ref, mixed_ref, keep_ref, send_ref, bias_ref,
):
    fill_bias(table_ref, bias_ref)
    size = n0.shape[0]
    for j, n in enumerate((n0, n1)):
        rows = slice(j * size, (j + 1) * size)
        for ref, w in ((q_ref, wq_ref), (k_ref, wk_ref), (v_ref, wv_ref)):
            ref[rows, :] = dot_nt(n[...], w[...]).astype(bf16)

    def step(i, carry):
        rows = pl.ds(pl.multiple_of(i * TGT_LEN, TGT_LEN), TGT_LEN)
        length = len_ref[(rank_ref[0] * (size // TGT_LEN)) ^ (base + i)]
        probs = self_probs(stack_heads(q_ref[rows, :]), k_ref[rows, :], bias_ref[...], length)
        mixed_ref[rows, :] = unstack_heads(dot_nn(probs.astype(bf16), v_ref[rows, :])).astype(bf16)
        return carry

    lax.fori_loop(0, 2 * size // TGT_LEN, step, 0, unroll=2)
    keep_ref[...] = dot_nn(mixed_ref[:size, :], wo_ref[...])
    send_ref[...] = dot_nn(mixed_ref[size:, :], wo_ref[...]).astype(bf16)


def store_parts(own_ref, chip_ref, send_ref, parts):
    for j, part in enumerate(parts):
        if j == 0:
            own_ref[...] = part
        elif j == 2:
            chip_ref[...] = part
        else:
            send_ref[j // 2] = part.astype(bf16)


def memory_forward(mem_ref, w0, w1, w2, w3, k_ref, v_ref):
    width = k_ref.shape[1] // 4
    half = mem_ref.shape[0] // 2
    blocks = (w0, w1, w2, w3)

    def step(i, carry):
        rows = pl.ds(pl.multiple_of(i * half, half), half)
        k_ref[rows, :] = dot_nt(mem_ref[rows, :], matrix(blocks, KEY, width)).astype(bf16)
        v_ref[rows, :] = dot_nt(mem_ref[rows, :], matrix(blocks, KEY + 1, width)).astype(bf16)
        return carry

    lax.fori_loop(0, 2, step, 0)


def cross_forward(
    x_ref, own_ref, near_ref, far_ref, k_ref, v_ref, gain_two_ref, gain_three_ref, w0, w1, w2, w3, w4, w5, rank_ref, len_ref, turn_ref,
    after_self_ref, n2_ref, q_ref, mixed_ref, after_ref, n3_ref,
):
    blocks = (w0, w1, w2, w3, w4, w5)
    first = first_of(turn_ref)
    after_self = x_ref[...].astype(f32) + own_ref[...] + near_ref[...].astype(f32) + far_ref[...].astype(f32)
    after_self_ref[...] = after_self
    normed = (after_self * row_scale(after_self) * gain_two_ref[...].reshape(1, -1)).astype(bf16)
    n2_ref[...] = normed
    q_ref[...] = dot_nt(normed, passed_on(blocks, first, 0)).astype(bf16)

    def probs(queries, key_rows, example, pair):
        return cross_probs(queries, key_rows, len_ref[rank_ref[0] * (q_ref.shape[0] // TGT_LEN) + example])

    attend(q_ref, k_ref, v_ref, mixed_ref, MEM_LEN, probs)
    after = after_self_ref[...] + dot_nn(mixed_ref[...], passed_on(blocks, first, 1))
    after_ref[...] = after
    n3_ref[...] = (after * row_scale(after) * gain_three_ref[...].reshape(1, -1)).astype(bf16)


def feed_hidden(c0, c1, c2, c3, out_ref, hidden_ref):
    size = c0.shape[0]
    for base, first, second in ((0, c0, c1), (2 * size, c2, c3)):

        def step(i, carry, base=base, first=first, second=second):
            rows = pl.ds(pl.multiple_of(base + i * size, size), size)
            hidden_ref[rows, :] = dot_nt(jnp.where(i == 0, first[...], second[...]), out_ref[...])
            return carry

        lax.fori_loop(0, 2, step, 0)


def feed_main(base, g0, g1, hidden_ref, in_ref, keep_ref, send_ref, act_ref, pre_grad_ref):
    size = g0.shape[0]
    for j, g in enumerate((g0, g1)):
        rows = slice(j * size, (j + 1) * size)
        pre = dot_nn(g[...], in_ref[...])
        square = pre * pre
        tanh = jnp.tanh(tanh_scale * (pre + cubic_term * square * pre))
        act_ref[rows, :] = (0.5 * pre * (1.0 + tanh)).astype(bf16)
        slope = 0.5 * (1.0 + tanh) + 0.5 * pre * (1.0 - tanh * tanh) * (
            tanh_scale * (1.0 + 3.0 * cubic_term * square)
        )
        low = (hidden_ref[base + j * size : base + (j + 1) * size, :] * slope).astype(bf16)
        pre_grad_ref[rows, :] = low
        grad = dot_nt(low, in_ref[...])
        if j == 0:
            keep_ref[...] = grad
        else:
            send_ref[...] = grad.astype(bf16)


def feed_rest(
    g0, g1, g2, g3, c0, c1, c2, c3, act_a, act_b, pre_grad_a, pre_grad_b, out_ref, turn_ref, own_ref, chip_ref, send_ref, low_ref, high_ref, grads_ref
):
    activated = jnp.concatenate([act_a[...], act_b[...]], 0)
    pre_grad = jnp.concatenate([pre_grad_a[...], pre_grad_b[...]], 0)
    gathered = jnp.concatenate([g[...] for g in (g0, g1, g2, g3)], 0)
    store_rows(grads_ref, (), 0, dot_tn(gathered, pre_grad), turn_ref[0])
    upstream = jnp.concatenate([c[...] for c in (c0, c1, c2, c3)], 0)
    store_rows(grads_ref, (), 1, dot_tn(activated, upstream), turn_ref[0])
    store_halves(low_ref, high_ref, grads_ref)
    size = g0.shape[0]
    for slot, act, keep_ref in ((0, act_a, own_ref), (1, act_b, chip_ref)):

        def step(i, carry, slot=slot, act=act, keep_ref=keep_ref):
            part = dot_nn(act[pl.ds(pl.multiple_of(i * size, size), size), :], out_ref[...])

            @pl.when(i == 0)
            def _():
                keep_ref[...] = part

            @pl.when(i == 1)
            def _():
                send_ref[slot] = part.astype(bf16)

            return carry

        lax.fori_loop(0, 2, step, 0)


def cross_backward(
    own_ref, near_ref, far_ref, cot_ref, after_ref, after_self_ref, gain_two_ref, gain_three_ref,
    n2_ref, q_ref, k_ref, v_ref, mixed_ref, w0, w1, w2, w3, w4, w5, rank_ref, len_ref, turn_ref,
    grad_one_ref, up_ref, dk_ref, dv_ref, gains_ref, keep_ref, send_ref, m_ref, dq_ref,
):
    blocks = (w0, w1, w2, w3, w4, w5)
    first = first_of(turn_ref)
    after = after_ref[...]
    scale = row_scale(after)
    upstream = own_ref[...] + near_ref[...].astype(f32) + far_ref[...].astype(f32)
    gains_ref[1:2, :] = jnp.sum(upstream * after * scale, 0, keepdims=True)
    grad_two = cot_ref[...].astype(f32) + norm_backward(after, scale, gain_three_ref[...].reshape(1, -1), upstream)
    grad_one_ref[...] = grad_two
    up_two = grad_two.astype(bf16)
    m_ref[...] = dot_nt(up_two, passed_on(blocks, first, 1)).astype(bf16)
    store_grad(keep_ref, send_ref, 1, dot_tn(mixed_ref[...], up_two), turn_ref[0])

    def probs(queries, key_rows, example, pair):
        return cross_probs(queries, key_rows, len_ref[rank_ref[0] * (q_ref.shape[0] // TGT_LEN) + example])

    attend_back(q_ref, k_ref, v_ref, m_ref, dq_ref, dk_ref, dv_ref, MEM_LEN, probs)
    store_grad(keep_ref, send_ref, 0, dot_tn(dq_ref[...], n2_ref[...]), turn_ref[0])
    upstream = dot_nn(dq_ref[...], passed_on(blocks, first, 0))
    hidden = after_self_ref[...]
    scale = row_scale(hidden)
    gains_ref[0:1, :] = jnp.sum(upstream * hidden * scale, 0, keepdims=True)
    grad_one = grad_one_ref[...] + norm_backward(hidden, scale, gain_two_ref[...].reshape(1, -1), upstream)
    grad_one_ref[...] = grad_one
    up_ref[...] = grad_one.astype(bf16)


def memory_weights(dk_ref, dv_ref, mem_ref, keep_in, send_in, late_ref, turn_ref, keep_ref, send_ref):
    count = keep_in.shape[2]
    late = jnp.concatenate([late_ref[...], jnp.zeros((EXTRA - 2, late_ref.shape[1]), f32)], 0)
    for j in range(2):
        for ref, given in ((keep_ref, keep_in), (send_ref, send_in)):
            for a in range(keep_in.shape[1]):
                ref[j, a, :count] = given[j, a]
            store_extra(ref, (j,), 2 * count, late, turn_ref[0])
    store_grad(keep_ref, send_ref, 2, dot_nn(dk_ref[...], mem_ref[...]), turn_ref[0])
    store_grad(keep_ref, send_ref, 3, dot_nn(dv_ref[...], mem_ref[...]), turn_ref[0])


def self_backward(
    u0, u1, u2, u3, n0, n1, n2, n3, qa, ka, va, xa, qb, kb, vb, xb, wq_ref, wk_ref, wv_ref, wo_ref, gain_ref,
    table_ref, rank_ref, len_ref, turn_ref,
    low_ref, high_ref, own_ref, chip_ref, send_ref,
    bias_ref, score_ref, m_ref, dq_ref, dk_ref, dv_ref, grads_ref,
):
    fill_bias(table_ref, bias_ref)
    score_ref[...] = jnp.zeros_like(score_ref)
    size = n0.shape[0]
    width = qa.shape[1]
    for j, u in enumerate((u0, u1, u2, u3)):
        m_ref[j * size : (j + 1) * size, :] = dot_nt(u[...], wo_ref[...]).astype(bf16)

    for base, q_ref, k_ref, v_ref in ((0, qa, ka, va), (2 * size, qb, kb, vb)):

        def step(i, carry, base=base, q_ref=q_ref, k_ref=k_ref, v_ref=v_ref):
            rows = pl.ds(pl.multiple_of(i * TGT_LEN, TGT_LEN), TGT_LEN)
            all_rows = pl.ds(pl.multiple_of(base + i * TGT_LEN, TGT_LEN), TGT_LEN)
            length = len_ref[(rank_ref[0] * (size // TGT_LEN)) ^ (base // TGT_LEN + i)]
            queries = stack_heads(q_ref[rows, :])
            grads = stack_heads(m_ref[all_rows, :])
            key_block = k_ref[rows, :]
            probs = self_probs(queries, key_block, bias_ref[...], length)
            dv_ref[all_rows, :] = dot_tn(probs.astype(bf16), grads).astype(bf16)
            prob_grad = dot_nt(grads, v_ref[rows, :])
            score_grad = probs * (prob_grad - jnp.sum(probs * prob_grad, -1, keepdims=True))
            score_ref[...] += score_grad
            low = score_grad.astype(bf16)
            dq_ref[all_rows, :] = unstack_heads(dot_nn(low, key_block)).astype(bf16)
            dk_ref[all_rows, :] = dot_tn(low, queries).astype(bf16)
            return carry

        lax.fori_loop(0, 2 * size // TGT_LEN, step, 0, unroll=2)
    normed = jnp.concatenate([n[...] for n in (n0, n1, n2, n3)], 0)
    upstream = jnp.concatenate([u[...] for u in (u0, u1, u2, u3)], 0)
    mixed = jnp.concatenate([xa[...], xb[...]], 0)
    for index, (left, right) in enumerate(
        ((dq_ref[...], normed), (dk_ref[...], normed), (dv_ref[...], normed), (mixed, upstream))
    ):
        store_rows(grads_ref, (), index, dot_tn(left, right), turn_ref[0])
    gain = jnp.zeros((1, n0.shape[1]), f32)
    parts = []
    for j, n in enumerate((n0, n1, n2, n3)):
        rows = slice(j * size, (j + 1) * size)
        part = dot_nn(dq_ref[rows, :], wq_ref[...])
        part = part + dot_nn(dk_ref[rows, :], wk_ref[...]) + dot_nn(dv_ref[rows, :], wv_ref[...])
        gain += jnp.sum(part * n[...].astype(f32), 0, keepdims=True)
        if j == 0:
            own_ref[...] = part
        elif j == 2:
            chip_ref[...] = part
        else:
            send_ref[j // 2] = part.astype(bf16)
    gain = gain * (1.0 / gain_ref[...].reshape(1, -1))
    heads = width // HEAD_DIM
    sums = [diagonal_sums(score_ref[h * TGT_LEN : (h + 1) * TGT_LEN, :]) for h in range(heads)]
    sums = jnp.concatenate(sums + [jnp.zeros((EXTRA - 1 - heads, TGT_LEN), f32)], 0)
    sums = jnp.concatenate([sums, jnp.zeros((EXTRA - 1, gain.shape[1] - TGT_LEN), f32)], 1)
    store_extra(grads_ref, (), 4 * (width // grads_ref.shape[0]), jnp.concatenate([gain, sums], 0), turn_ref[0])
    store_halves(low_ref, high_ref, grads_ref)


def last_norm(grad_one_ref, own_ref, near_ref, far_ref, x_ref, gain_ref, grad_ref):
    upstream = own_ref[...] + near_ref[...].astype(f32) + far_ref[...].astype(f32)
    hidden = x_ref[...].astype(f32)
    grad_ref[...] = grad_one_ref[...] + norm_backward(hidden, row_scale(hidden), gain_ref[...].reshape(1, -1), upstream)


def gather_order(bits, early):
    return [0, bits - 1, *range(1, bits - 1)] if early else list(range(bits))


def gather_rows(low_ref, high_ref, rows, places, turn, early):
    half = low_ref.shape[0]
    order = gather_order((2 * half).bit_length() - 1, early)
    pieces = []
    for a in places:
        place = a ^ turn
        inside = sum(((place >> bit) & 1) << i for i, bit in enumerate(order[:-1]))
        low = (place >> order[-1]) & 1 == 0
        pieces.append(jnp.where(low, low_ref[inside, rows].astype(f32), high_ref[inside, rows].astype(f32)))
    return jnp.concatenate(pieces, 0)


def finish(early, low_ref, high_ref, turn_ref, *outs):
    blocks = 2 * low_ref.shape[0]
    start = 0
    for ref in outs:
        extra = ref.shape[0] == EXTRA
        places = range(1) if extra else range(blocks)
        size = EXTRA if extra else ref.shape[0] // blocks
        ref[...] = gather_rows(low_ref, high_ref, slice(start, start + size), places, turn_ref[0], early)
        start += size


def memory_backward(dk_ref, dv_ref, w0, w1, w2, w3, grad_ref):
    blocks = (w0, w1, w2, w3)
    width = dk_ref.shape[0] // 4
    half = grad_ref.shape[0] // 2

    def step(i, carry):
        rows = pl.ds(pl.multiple_of(i * half, half), half)
        keys = dot_tn(dk_ref[:, rows], matrix(blocks, KEY, width))
        grad_ref[rows, :] = keys + dot_tn(dv_ref[:, rows], matrix(blocks, KEY + 1, width))
        return carry

    lax.fori_loop(0, 2, step, 0)


KEY = 0


def call(kernel, operands, outs, scratch=(), flops=0, smem=()):
    moved = sum(a.size * a.dtype.itemsize for a in operands)
    moved += sum(functools.reduce(lambda x, y: x * y, s) * jnp.dtype(t).itemsize for s, t in outs)
    return pl.pallas_call(
        kernel,
        out_shape=[jax.ShapeDtypeStruct(s, t) for s, t in outs],
        in_specs=[
            pl.BlockSpec(memory_space=pltpu.SMEM if i in smem else pltpu.VMEM) for i in range(len(operands))
        ],
        out_specs=[pl.BlockSpec(memory_space=pltpu.VMEM) for _ in outs],
        scratch_shapes=[pltpu.VMEM(s, t) for s, t in scratch],
        compiler_params=pltpu.CompilerParams(vmem_limit_bytes=VMEM_LIMIT),
        cost_estimate=pl.CostEstimate(flops=flops, bytes_accessed=moved, transcendentals=0),
    )(*operands)


VMEM_LIMIT = 56 * 1024 * 1024


def after(value, *others):
    return lax.optimization_barrier((value, *others))[0]


def swap_core(a):
    return lax.ppermute(a, "mp", [(0, 1), (1, 0), (2, 3), (3, 2)])


def swap_chip(a):
    return lax.ppermute(a, "mp", [(0, 2), (2, 0), (1, 3), (3, 1)])


def gather_blocks(a):
    far = swap_chip(a)
    return (a, swap_core(a), far, swap_core(far))


def core_sum(chip, got):
    return (chip.astype(f32) + got.astype(f32)).astype(bf16)


def plus(a, b):
    return (a.astype(f32) + b.astype(f32)).astype(bf16)


def swap_dp(a, bit):
    return lax.ppermute(a, "dp", [(i, i ^ (1 << bit)) for i in range(lax.axis_size("dp"))])


def dp_chain(keep, send, steps=None):
    bits = lax.axis_size("dp").bit_length() - 1
    for bit in range(bits):
        got = swap_dp(send, bit)
        tokens = yield send
        got = after(got, *tokens)
        half = keep.shape[0] // 2
        if half:
            send, keep = plus(keep[half:], got[half:]), plus(keep[:half], got[:half])
        else:
            value = plus(keep, got)
    yield from gather_chain(value, range(bits)[:steps])


def gather_chain(value, order):
    bits = lax.axis_size("dp").bit_length() - 1
    order = list(order)
    for bit in order:
        other = swap_dp(value, bits - 1 - bit)
        tokens = yield value
        other = after(other, *tokens)
        if bit != order[-1]:
            value = jnp.concatenate([value, other], 0)
    yield value, other


ROUNDS = (
    ("zero",),
    ("two",),
    ("two",),
    ("zero", "one"),
    ("two", "one"),
)
LATE_ROUNDS = (
    ("two", "one"),
    ("in", "out"),
    ("two",),
    ("one",),
)
FINISH = ("in", "out", "one", "two", "one+")


class Chains:
    def __init__(self):
        self.under_way, self.last, self.tokens = {}, {}, ()

    def start(self, name, chain):
        self.under_way[name] = chain
        self.last[name] = next(chain)
        return self.last[name]

    def turn(self, *names):
        sent = []
        for name in names:
            try:
                self.last[name] = self.under_way[name].send(self.tokens)
                sent.append(self.last[name])
            except (StopIteration, KeyError):
                self.under_way.pop(name, None)
        if sent:
            self.tokens = tuple(t for t in sent if not isinstance(t, tuple)) or sent[0]
        return self.tokens

    def drain(self):
        while self.under_way:
            for name in list(self.under_way):
                self.turn(name)


def body(
    inputs,
    memory,
    target_len,
    memory_len,
    bucket_map,
    self_gain,
    self_query,
    self_key,
    self_value,
    self_out,
    bias_table,
    cross_gain,
    cross_query,
    cross_key,
    cross_value,
    cross_out,
    feed_gain,
    feed_input,
    feed_output,
    cotangent,
):
    rank = lax.axis_index("mp")
    rows, d = inputs.shape
    key_rows = memory.shape[0]
    width = self_query.shape[1]
    wide = 4 * width
    heads = bias_table.shape[1]
    units = feed_input.shape[1]
    examples = rows // TGT_LEN
    rank_value = rank.astype(jnp.int32).reshape(1)
    blocks = lax.axis_size("dp")
    place = lax.axis_index("dp").astype(jnp.int32)
    turn = jnp.zeros((1,), jnp.int32)
    for bit in range(blocks.bit_length() - 1):
        turn = 2 * turn + ((place >> bit) & 1)
    turn = jnp.concatenate([turn, (place & 1).reshape(1)])

    distance = (TGT_LEN - jnp.arange(TGT_LEN, dtype=jnp.int32)) % TGT_LEN
    lookup = distance[:, None] == jnp.arange(TGT_LEN, dtype=jnp.int32)[None, :]
    bucket = jnp.sum(jnp.where(lookup, bucket_map[None, :], 0), -1)
    hot = (bucket[:, None] == jnp.arange(BUCKETS, dtype=jnp.int32)[None, :]).astype(f32)
    by_distance = lax.dot_general(bias_table, hot, (((0,), (1,)), ((), ())), precision=highest)
    big = (rows, d)
    head_rows = (rows, wide)
    key_heads = (key_rows, wide)
    heads_key = (wide, key_rows)
    square = ((heads * TGT_LEN, TGT_LEN), f32)
    group_heads = (4 * rows, width)
    half_heads = (2 * rows, width)
    pack = ((2, rows, d), bf16)
    product = 2 * rows * d * wide

    def grad_half(count, size, more=0):
        return ((blocks // 2, count * (size // blocks) + more, d), bf16)

    def grad_rows(count, size, lead=(), more=0):
        return ((*lead, blocks, count * (size // blocks) + more, d), bf16)

    pair_own = jnp.concatenate([cross_key.T, cross_value.T], 0)
    query_own = jnp.concatenate([cross_query.T, cross_out], 0)
    half_own = lax.dynamic_slice_in_dim(query_own, (place & 1) * width, width, 0)
    normed_one = call(first_norm, (inputs, self_gain), [(big, bf16)])[0]
    far = swap_chip(normed_one)
    pair_far = swap_chip(after(pair_own, normed_one))
    self_weights = (self_query.T, self_key.T, self_value.T, self_out)

    def self_half(base, pair):
        return call(
            functools.partial(self_forward, base),
            (*pair, *self_weights, by_distance, rank_value, target_len),
            [(half_heads, bf16)] * 4 + [(big, f32), (big, bf16)],
            [square],
            flops=2 * product,
            smem=(7, 8),
        )

    ones = (normed_one, swap_core(normed_one))
    *self_a, own, send = self_half(0, ones)
    near = swap_core(send)
    far = after(far, near)
    ones = (*ones, far, swap_core(far))
    *self_b, chip, send = self_half(2 * rows // TGT_LEN, ones[2:])
    pair_far = after(pair_far, chip)
    half_far = swap_chip(after(half_own, normed_one))
    far_send = core_sum(chip, swap_core(after(send, pair_far)))
    far = swap_chip(far_send)
    pair = (pair_own, swap_core(pair_own), pair_far, swap_core(pair_far))
    cross_k, cross_v = call(
        memory_forward, (after(memory, far_send), *pair), [(key_heads, bf16)] * 2, flops=8 * product
    )
    half_far = after(half_far, cross_v)
    half_passed = swap_dp(half_far, 0)
    far = after(far, half_far)
    half_passed = after(half_passed, far)
    query = (query_own, swap_core(query_own), half_far, half_passed, swap_core(half_far), swap_core(half_passed))
    ups_far = swap_chip(after(cotangent, far))
    after_self, normed_two, cross_q, cross_mixed, after_cross, normed_three = call(
        cross_forward,
        (inputs, own, near, far, cross_k, cross_v, cross_gain, feed_gain, *query, rank_value, memory_len, turn),
        [(big, f32), (big, bf16), (head_rows, bf16), (head_rows, bf16), (big, f32), (big, bf16)],
        flops=6 * product,
        smem=(14, 15, 16),
    )
    ups_far = after(ups_far, normed_three)
    ups = (cotangent, swap_core(cotangent), ups_far, swap_core(ups_far))
    many = 4 * rows
    far = swap_chip(normed_three)
    hidden = call(feed_hidden, (*ups, feed_output), [((many, units), f32)], flops=4 * product)[0]

    def feed_half(base, pair):
        return call(
            functools.partial(feed_main, base),
            (*pair, hidden, feed_input),
            [(big, f32), (big, bf16), ((2 * rows, units), bf16), ((2 * rows, units), bf16)],
            flops=4 * product,
        )

    gathered = (normed_three, swap_core(normed_three))
    own, send, act_a, pre_grad_a = feed_half(0, gathered)
    near = swap_core(send)
    far = after(far, near)
    gathered = (*gathered, far, swap_core(far))
    chip, send, act_b, pre_grad_b = feed_half(2 * rows, gathered[2:])
    far_send = core_sum(chip, swap_core(send))
    far = swap_chip(far_send)
    out_own, out_chip, out_send, low, high = call(
        feed_rest,
        (*gathered, *ups, act_a, after(act_b, far_send), pre_grad_a, pre_grad_b, feed_output, turn),
        [(big, f32), (big, f32), pack] + [grad_half(2, d)] * 2,
        [grad_rows(2, d)],
        flops=12 * product,
        smem=(13,),
    )
    chains = Chains()
    token = chains.start("zero", dp_chain(low, high, steps=1))
    far = after(far, token)
    grad_one, up_one, key_grad, value_grad, late_gains, keep, send = call(
        cross_backward,
        (own, near, far, cotangent, after_cross, after_self, cross_gain, feed_gain)
        + (normed_two, cross_q, cross_k, cross_v, cross_mixed, *query, rank_value, memory_len, turn),
        [(big, f32), (big, bf16), (heads_key, bf16), (heads_key, bf16), ((2, d), f32)] + [grad_rows(2, width, (2,))] * 2,
        [(head_rows, bf16), (head_rows, bf16)],
        flops=16 * product,
        smem=(19, 20, 21),
    )
    up_far = swap_chip(up_one)
    keep, send = call(
        memory_weights,
        (key_grad, value_grad, memory, keep, send, late_gains, turn),
        [grad_rows(4, width, (2,), EXTRA)] * 2,
        flops=8 * product,
        smem=(6,),
    )
    up_far = after(up_far, keep)
    chains.tokens = (up_far,)
    token = chains.turn("zero")
    got = swap_core(after(send, *token))
    one_send = core_sum(keep[1], got[1])
    one_far = swap_chip(one_send)
    self_ups = (up_one, swap_core(up_one), after(up_far, one_send), swap_core(up_far))
    low, high, own, chip, send = call(
        self_backward,
        (*self_ups, *ones, *self_a, *self_b)
        + (*self_weights, self_gain, by_distance, rank_value, target_len, turn),
        [grad_half(4, width, EXTRA)] * 2 + [(big, f32), (big, f32), pack],
        [square, square] + [(group_heads, bf16)] * 4 + [grad_rows(4, width, (), EXTRA)],
        flops=10 * product,
        smem=(22, 23, 24),
    )
    chains.tokens = (own,)
    token = chains.turn("zero")
    token = chains.start("two", dp_chain(low, after(high, *token)))
    got_self = swap_core(after(send, token))
    far_send = core_sum(chip, got_self[1])
    far = swap_chip(far_send)
    one_sum = keep[0].astype(f32) + got[0].astype(f32) + after(one_far, far_send).astype(f32)
    one_sum = one_sum.astype(bf16)
    token = chains.start("one", dp_chain(one_sum[: blocks // 2], one_sum[blocks // 2 :]))
    memory_grad = call(
        memory_backward,
        (after(key_grad, token), value_grad, *pair),
        [((key_rows, d), f32)],
        flops=8 * product,
    )[0]
    chains.tokens = (memory_grad,)
    more = blocks.bit_length() - 1 - 3
    for _ in range(more):
        chains.turn("zero")
    for names in ROUNDS:
        chains.turn(*names)
        if "feed" not in chains.last and isinstance(chains.last["zero"], tuple):
            bits = blocks.bit_length() - 1
            both = jnp.concatenate(chains.last["zero"], 0)
            half = both.shape[1] // 2
            chains.last["feed"] = None
            chains.start("in", gather_chain(both[:, :half], gather_order(bits, True)[1:]))
            chains.start("out", gather_chain(both[:, half:], gather_order(bits, False)[1:]))
    inputs_grad = call(
        last_norm,
        (grad_one, own, got_self[0], after(far, *chains.tokens), inputs, self_gain),
        [(big, f32)],
    )[0]
    chains.tokens = (inputs_grad,)
    got_out = swap_core(after(out_send, *chains.tokens))
    out_far = swap_chip(core_sum(out_chip, got_out[1]))
    for _ in range(2 * more):
        chains.turn("two", "one")
    for names in LATE_ROUNDS:
        chains.turn(*names)
    grads = {}
    for name in FINISH:
        if name == "in":
            for _ in range(more):
                chains.turn("in", "out")
            chains.turn("in", "out")
        elif name == "one":
            chains.turn("one")
            continue
        elif name == "two":
            chains.turn("two", "one")
        name = name.strip("+")
        feed = name in ("in", "out")
        outs = [((d, d), f32)] if feed else [((width, d), f32)] * 4 + [((EXTRA, d), f32)]
        grads[name] = call(
            functools.partial(finish, name == "in"), (*chains.last[name], turn), outs, smem=(2,)
        )
        if feed or name == "one":
            chains.tokens = (grads[name][-1],)
    extra = grads["two"][-1]
    gain_one = after(extra[:1], *chains.tokens)
    gain_one = gain_one + swap_core(gain_one)
    gain_one = gain_one + swap_chip(gain_one)
    layer_out = (after_cross + out_own + got_out[0].astype(f32) + out_far.astype(f32)).astype(bf16)
    feed_grads, cross_grads, self_grads = (grads["in"][0], grads["out"][0]), grads["one"], grads["two"]
    own_sums = extra[1 : 1 + heads, :TGT_LEN]
    bias_grad = lax.dot_general(hot, own_sums, (((0,), (1,)), ((), ())), precision=highest)

    return (
        layer_out,
        inputs_grad,
        memory_grad,
        gain_one[0],
        self_grads[0].T,
        self_grads[1].T,
        self_grads[2].T,
        self_grads[3],
        bias_grad,
        cross_grads[4][0],
        cross_grads[0].T,
        cross_grads[2].T,
        cross_grads[3].T,
        cross_grads[1],
        cross_grads[4][1],
        *feed_grads,
    )


def solution(mesh):
    in_specs = (
        P(("dp", "mp"), None),
        P(("dp", "mp"), None),
        P("dp"),
        P("dp"),
        P(),
        P(),
        P(None, "mp"),
        P(None, "mp"),
        P(None, "mp"),
        P("mp", None),
        P(None, "mp"),
        P(),
        P(None, "mp"),
        P(None, "mp"),
        P(None, "mp"),
        P("mp", None),
        P(),
        P(None, "mp"),
        P("mp", None),
        P(("dp", "mp"), None),
    )
    out_specs = (
        P(("dp", "mp"), None),
        P(("dp", "mp"), None),
        P(("dp", "mp"), None),
        P(),
        P(None, "mp"),
        P(None, "mp"),
        P(None, "mp"),
        P("mp", None),
        P(None, "mp"),
        P(),
        P(None, "mp"),
        P(None, "mp"),
        P(None, "mp"),
        P("mp", None),
        P(),
        P(None, "mp"),
        P("mp", None),
    )
    return jax.shard_map(body, mesh=mesh, in_specs=in_specs, out_specs=out_specs, check_vma=False)
```

profile of v0, /device:TPU:0, one launch (start us, length us, event | category | flops | bytes accessed | tf_op | source)
XLA Modules:
  0.0 275.4 jit_solution(13599409063508711973)
XLA Ops:
  0.7 1.9 shard_map.323.n0
  2.6 2.9 %collective-permute-start.2 = (bf16[256,768]{1,0:T(8,128)(2,1)}, bf16[256,768]{1,0:T(8,128)(2,1)S(1)}, u32[]{:S(2)}, u32[]{:S(2)}) collective-permute-start(bf16[256,768]{1,0:T(8,128)(2,1)} %shard_map.323.n0), channel_id=1, source_target_pairs={{0,2},{2,0},{1,3},{3,1},{4,6},{6,4},{5,7},{7,5},{8,10},{10,8},{9,1... | collective-permute-start | bytes 1179656 | tf_op jit(solution)/shard_map/ppermute | solution.py:519
  8.2 5.6 %shard_map.324 = (bf16[512,192]{1,0:T(8,128)(2,1)}, bf16[512,192]{1,0:T(8,128)(2,1)}, bf16[512,192]{1,0:T(8,128)(2,1)}, bf16[512,192]{1,0:T(8,128)(2,1)}, f32[256,768]{1,0:T(8,128)}, /*index=5*/bf16[256,768]{1,0:T(8,128)(2,1)}) custom-call(bf16[256,768]{1,0:T(8,128)(2,1)} %shard_map.323.n0, bf16[256,768]{1,0:T(8,128)(2,1)} %copy-done.42, ...), custom_call_target="tpu_custom_call" | custom-call | flops 603979776 | bytes 3933732 | tf_op jit(solution)/shard_map/pallas_call | solution.py:494
  18.3 5.6 %shard_map.325 = (bf16[512,192]{1,0:T(8,128)(2,1)}, bf16[512,192]{1,0:T(8,128)(2,1)}, bf16[512,192]{1,0:T(8,128)(2,1)}, bf16[512,192]{1,0:T(8,128)(2,1)}, f32[256,768]{1,0:T(8,128)}, /*index=5*/bf16[256,768]{1,0:T(8,128)(2,1)}) custom-call(bf16[256,768]{1,0:T(8,128)(2,1)} %copy-done.41, bf16[256,768]{1,0:T(8,128)(2,1)} %copy-done.43, ...), custom_call_target="tpu_custom_call" | custom-call | flops 603979776 | bytes 3933732 | tf_op jit(solution)/shard_map/pallas_call | solution.py:494
  23.9 6.0 %collective-permute-done.4.w2 = bf16[384,768]{1,0:T(8,128)(2,1)} collective-permute-done((bf16[384,768]{1,0:T(8,128)(2,1)S(1)}, bf16[384,768]{1,0:T(8,128)(2,1)}, u32[]{:S(2)}, u32[]{:S(2)}) %collective-permute-start.4) | collective-permute-done | bytes 589856 | tf_op jit(solution)/shard_map/ppermute | solution.py:519
  33.6 6.2 %shard_map.326 = (bf16[1024,768]{1,0:T(8,128)(2,1)}, bf16[1024,768]{1,0:T(8,128)(2,1)}) custom-call(bf16[1024,768]{1,0:T(8,128)(2,1)} %mem_ref.2, bf16[384,768]{1,0:T(8,128)(2,1)} %copy-done.22, bf16[384,768]{1,0:T(8,128)(2,1)} %collective-permute-done.8.w1, bf16[384,768]{1,0:T(8,128)(2,1)} %collective-permute-done.4.w2, ...), custom_call_target="tpu_custom_call" | custom-call | flops 2415919104 | bytes 7077888 | tf_op jit(solution)/shard_map/pallas_call | solution.py:494
  42.7 5.9 %collective-permute-done.6.far_ref = bf16[256,768]{1,0:T(8,128)(2,1)S(1)} collective-permute-done((bf16[256,768]{1,0:T(8,128)(2,1)S(1)}, bf16[256,768]{1,0:T(8,128)(2,1)S(1)}, u32[]{:S(2)}, u32[]{:S(2)}) %collective-permute-start.6) | collective-permute-done | bytes 393248 | tf_op jit(solution)/shard_map/ppermute | solution.py:519
  51.2 11.4 %shard_map.327 = (f32[256,768]{1,0:T(8,128)}, bf16[256,768]{1,0:T(8,128)(2,1)}, bf16[256,768]{1,0:T(8,128)(2,1)}, bf16[256,768]{1,0:T(8,128)(2,1)}, f32[256,768]{1,0:T(8,128)}, /*index=5*/bf16[256,768]{1,0:T(8,128)(2,1)}) custom-call(bf16[256,768]{1,0:T(8,128)(2,1)} %x_ref.5, f32[256,768]{1,0:T(8,128)} %get-tuple-element.118.own_ref, ...), custom_call_target="tpu_custom_call" | custom-call | flops 1811939328 | bytes 10623020 | tf_op jit(solution)/shard_map/pallas_call | solution.py:494
  66.1 5.6 %shard_map.328.hidden_ref = f32[1024,768]{1,0:T(8,128)} custom-call(bf16[256,768]{1,0:T(8,128)(2,1)} %cot_ref.1, bf16[256,768]{1,0:T(8,128)(2,1)} %copy-done.29, bf16[256,768]{1,0:T(8,128)(2,1)} %copy-done.28, bf16[256,768]{1,0:T(8,128)(2,1)} %copy-done.30, bf16[768,768]{1,0:T(8,128)(2,1)} %out_ref.3), custom_call_target="tpu_custom_call" | custom-call | flops 1207959552 | bytes 5898240 | tf_op jit(solution)/shard_map/pallas_call | solution.py:494
  72.5 5.5 %shard_map.329 = (f32[256,768]{1,0:T(8,128)}, bf16[256,768]{1,0:T(8,128)(2,1)}, bf16[512,768]{1,0:T(8,128)(2,1)}, bf16[512,768]{1,0:T(8,128)(2,1)}) custom-call(bf16[256,768]{1,0:T(8,128)(2,1)} %get-tuple-element.134.g0, bf16[256,768]{1,0:T(8,128)(2,1)} %copy-done.31, f32[1024,768]{1,0:T(8,128)} %shard_map.328.hidden_ref, bf16[768,768]{1,0:T(8,128)(2,1)} %in_ref.3), custom_call_target="tpu_custom_call" | custom-call | flops 1207959552 | bytes 7864320 | tf_op jit(solution)/shard_map/pallas_call | solution.py:494
  78.1 1.9 collective-permute-done.19.near_ref
  80.1 1.6 collective-permute-done.20.g1.g3
  82.4 5.6 %shard_map.330 = (f32[256,768]{1,0:T(8,128)}, bf16[256,768]{1,0:T(8,128)(2,1)}, bf16[512,768]{1,0:T(8,128)(2,1)}, bf16[512,768]{1,0:T(8,128)(2,1)}) custom-call(bf16[256,768]{1,0:T(8,128)(2,1)} %copy-done.32, bf16[256,768]{1,0:T(8,128)(2,1)} %copy-done.33, f32[1024,768]{1,0:T(8,128)} %shard_map.328.hidden_ref, bf16[768,768]{1,0:T(8,128)(2,1)} %in_ref.3), custom_call_target="tpu_custom_call" | custom-call | flops 1207959552 | bytes 7864320 | tf_op jit(solution)/shard_map/pallas_call | solution.py:494
  88.2 1.8 collective-permute-done.21
  91.9 10.2 %shard_map.331 = (f32[256,768]{1,0:T(8,128)}, f32[256,768]{1,0:T(8,128)}, bf16[2,256,768]{2,1,0:T(8,128)(2,1)}, bf16[4,192,768]{2,1,0:T(8,128)(2,1)}, bf16[4,192,768]{2,1,0:T(8,128)(2,1)}) custom-call(bf16[256,768]{1,0:T(8,128)(2,1)} %get-tuple-element.134.g0, bf16[256,768]{1,0:T(8,128)(2,1)} %copy-done.31, bf16[256,768]{1,0:T(8,128)(2,1)} %copy-done.32, ...), custom_call_target="tpu_custom_call" | custom-call | flops 3623878656 | bytes 12189704 | tf_op jit(solution)/shard_map/pallas_call | solution.py:494
  102.1 1.6 collective-permute-start.25
  104.4 18.1 %shard_map.332 = (f32[256,768]{1,0:T(8,128)}, bf16[256,768]{1,0:T(8,128)(2,1)}, bf16[768,1024]{1,0:T(8,128)(2,1)}, bf16[768,1024]{1,0:T(8,128)(2,1)}, f32[2,768]...) custom-call(f32[256,768]{1,0:T(8,128)} %get-tuple-element.148.own_ref, ...), custom_call_target="tpu_custom_call" | custom-call | flops 4831838208 | bytes 16920620 | tf_op jit(solution)/shard_map/pallas_call | solution.py:494
  124.0 8.0 %shard_map.333 = (bf16[2,8,104,768]{3,2,1,0:T(8,128)(2,1)}, bf16[2,8,104,768]{3,2,1,0:T(8,128)(2,1)}) custom-call(bf16[768,1024]{1,0:T(8,128)(2,1)} %get-tuple-element.186.dk_ref, bf16[768,1024]{1,0:T(8,128)(2,1)} %get-tuple-element.158.dv_ref, bf16[1024,768]{1,0:T(8,128)(2,1)} %mem_ref.2, bf16[2,8,48,768]{3,2,1,0:T(8,128)(2,1)} %get-tuple-element.159.keep_in, ...), custom_call_target="tpu_custom_call" | custom-call | flops 2415919104 | bytes 12195848 | tf_op jit(solution)/shard_map/pallas_call | solution.py:494
  135.1 1.6 collective-permute-start.28
  136.7 3.5 %collective-permute-done.26 = bf16[2,8,104,768]{3,2,1,0:T(8,128)(2,1)S(1)} collective-permute-done((bf16[2,8,104,768]{3,2,1,0:T(8,128)(2,1)}, bf16[2,8,104,768]{3,2,1,0:T(8,128)(2,1)S(1)}, u32[]{:S(2)}, u32[]{:S(2)}) %collective-permute-start.26) | collective-permute-done | bytes 2555936 | tf_op jit(solution)/shard_map/ppermute | solution.py:515
  143.5 13.9 %shard_map.334 = (bf16[4,104,768]{2,1,0:T(8,128)(2,1)}, bf16[4,104,768]{2,1,0:T(8,128)(2,1)}, f32[256,768]{1,0:T(8,128)}, f32[256,768]{1,0:T(8,128)}, bf16[2,256,768]{2,1,0:T(8,128)(2,1)}) custom-call(bf16[256,768]{1,0:T(8,128)(2,1)} %get-tuple-element.156.u0, bf16[256,768]{1,0:T(8,128)(2,1)} %copy-done.47, bf16[256,768]{1,0:T(8,128)(2,1)} %collective-permute-done.24.u2, ...), custom_call_target="tpu_custom_call" | custom-call | flops 3019898880 | bytes 9540140 | tf_op jit(solution)/shard_map/pallas_call | solution.py:494
  157.4 1.8 add_convert_fusion.11
  159.3 2.6 collective-permute-start.32
  163.4 7.3 %collective-permute-done.33 = bf16[8,104,768]{2,1,0:T(8,128)(2,1)S(1)} collective-permute-done((bf16[8,104,768]{2,1,0:T(8,128)(2,1)S(1)}, bf16[8,104,768]{2,1,0:T(8,128)(2,1)S(1)}, u32[]{:S(2)}, u32[]{:S(2)}) %collective-permute-start.33) | collective-permute-done | bytes 1277984 | tf_op jit(solution)/shard_map/ppermute | solution.py:519
  171.8 7.3 %shard_map.335 = f32[1024,768]{1,0:T(8,128)} custom-call(bf16[768,1024]{1,0:T(8,128)(2,1)} %get-tuple-element.186.dk_ref, bf16[768,1024]{1,0:T(8,128)(2,1)} %get-tuple-element.158.dv_ref, bf16[384,768]{1,0:T(8,128)(2,1)} %copy-done.22, bf16[384,768]{1,0:T(8,128)(2,1)} %collective-permute-done.8.w1, bf16[384,768]{1,0:T(8,128)(2,1)} %collective-permute-done.4.w2, ...), custom_call_target="tpu_custom_call" | custom-call | flops 2415919104 | bytes 8650752 | tf_op jit(solution)/shard_map/pallas_call | solution.py:494
  181.7 1.6 collective-permute-start.34
  184.7 2.6 collective-permute-start.42
  187.3 8.7 %collective-permute-done.34 = bf16[2,104,768]{2,1,0:T(8,128)(2,1)S(1)} collective-permute-done((bf16[2,104,768]{2,1,0:T(8,128)(2,1)S(1)}, bf16[2,104,768]{2,1,0:T(8,128)(2,1)S(1)}, u32[]{:S(2)}, u32[]{:S(2)}) %collective-permute-start.34) | collective-permute-done | bytes 319520 | tf_op jit(solution)/shard_map/ppermute | solution.py:536
  196.8 2.5 collective-permute-start.37
  200.1 3.3 %collective-permute-done.42 = bf16[1,192,768]{2,1,0:T(8,128)(2,1)S(1)} collective-permute-done((bf16[1,192,768]{2,1,0:T(8,128)(2,1)S(1)}, bf16[1,192,768]{2,1,0:T(8,128)(2,1)S(1)}, u32[]{:S(2)}, u32[]{:S(2)}) %collective-permute-start.42) | collective-permute-done | bytes 294944 | tf_op jit(solution)/shard_map/ppermute | solution.py:536
  203.4 3.0 %collective-permute-done.35 = bf16[1,104,768]{2,1,0:T(8,128)(2,1)S(1)} collective-permute-done((bf16[1,104,768]{2,1,0:T(8,128)(2,1)S(1)}, bf16[1,104,768]{2,1,0:T(8,128)(2,1)S(1)}, u32[]{:S(2)}, u32[]{:S(2)}) %collective-permute-start.35) | collective-permute-done | bytes 159776 | tf_op jit(solution)/shard_map/ppermute | solution.py:536
  206.6 2.5 collective-permute-done.37
  210.5 2.0 collective-permute-start.45
  214.9 3.1 %shard_map.336 = f32[256,768]{1,0:T(8,128)} custom-call(f32[256,768]{1,0:T(8,128)} %get-tuple-element.155.grad_one_ref, f32[256,768]{1,0:T(8,128)} %get-tuple-element.177.own_ref, bf16[256,768]{1,0:T(8,128)(2,1)} %slice_bitcast_fusion.3.near_ref, bf16[256,768]{1,0:T(8,128)(2,1)} %copy-done.35, bf16[256,768]{1,0:T(8,128)(2,1)} %x_ref.5, f32[768]{0:T(1024)} %gain_ref.5), custom_call_target="tpu_custom_call" | custom-call | bytes 3542016 | tf_op jit(solution)/shard_map/pallas_call | solution.py:494
  219.7 3.0 %collective-permute-done.44 = bf16[1,104,768]{2,1,0:T(8,128)(2,1)S(1)} collective-permute-done((bf16[1,104,768]{2,1,0:T(8,128)(2,1)S(1)}, bf16[1,104,768]{2,1,0:T(8,128)(2,1)S(1)}, u32[]{:S(2)}, u32[]{:S(2)}) %collective-permute-start.44) | collective-permute-done | bytes 159776 | tf_op jit(solution)/shard_map/ppermute | solution.py:536
  222.8 2.7 collective-permute-done.45
  225.5 1.6 collective-permute-start.49
  227.2 7.2 %collective-permute-done.41 = bf16[2,104,768]{2,1,0:T(8,128)(2,1)S(1)} collective-permute-done((bf16[2,104,768]{2,1,0:T(8,128)(2,1)S(1)}, bf16[2,104,768]{2,1,0:T(8,128)(2,1)S(1)}, u32[]{:S(2)}, u32[]{:S(2)}) %collective-permute-start.41) | collective-permute-done | bytes 319520 | tf_op jit(solution)/shard_map/ppermute | solution.py:536
  234.6 1.6 collective-permute-start.46
  236.2 1.9 collective-permute-start.53
  238.1 2.2 collective-permute-done.49.high_ref
  241.1 2.9 %shard_map.337 = f32[768,768]{1,0:T(8,128)} custom-call(bf16[4,96,768]{2,1,0:T(8,128)(2,1)} %copy-done.7, bf16[4,96,768]{2,1,0:T(8,128)(2,1)} %copy-done.24, s32[2]{0:T(128)} %pad_add_fusion.turn_ref), custom_call_target="tpu_custom_call" | custom-call | bytes 3538952 | tf_op jit(solution)/shard_map/pallas_call | solution.py:494
  246.8 3.7 %collective-permute-start.39 = (bf16[256,768]{1,0:T(8,128)(2,1)S(1)}, bf16[256,768]{1,0:T(8,128)(2,1)S(1)}, u32[]{:S(2)}, u32[]{:S(2)}) collective-permute-start(bf16[256,768]{1,0:T(8,128)(2,1)S(1)} %fusion.2), channel_id=1, source_target_pairs={{0,2},{2,0},{1,3},{3,1},{4,6},{6,4},{5,7},{7,5},{8,10},{10,8},{9,1... | collective-permute-start | bytes 1179656 | tf_op jit(solution)/shard_map/ppermute | solution.py:519
  250.5 4.5 %collective-permute-done.53.high_ref = bf16[4,96,768]{2,1,0:T(8,128)(2,1)S(1)} collective-permute-done((bf16[4,96,768]{2,1,0:T(8,128)(2,1)S(1)}, bf16[4,96,768]{2,1,0:T(8,128)(2,1)S(1)}, u32[]{:S(2)}, u32[]{:S(2)}) %collective-permute-start.53) | collective-permute-done | bytes 589856 | tf_op jit(solution)/shard_map/ppermute | solution.py:536
  255.8 2.9 %shard_map.340 = f32[768,768]{1,0:T(8,128)} custom-call(bf16[4,96,768]{2,1,0:T(8,128)(2,1)} %copy-done.6, bf16[4,96,768]{2,1,0:T(8,128)(2,1)} %copy-done.23, s32[2]{0:T(128)} %pad_add_fusion.turn_ref), custom_call_target="tpu_custom_call" | custom-call | bytes 3538952 | tf_op jit(solution)/shard_map/pallas_call | solution.py:494
  259.6 2.9 %shard_map.338 = (f32[192,768]{1,0:T(8,128)}, f32[192,768]{1,0:T(8,128)}, f32[192,768]{1,0:T(8,128)}, f32[192,768]{1,0:T(8,128)}, f32[8,768]{1,0:T(8,128)}) custom-call(bf16[4,104,768]{2,1,0:T(8,128)(2,1)} %copy-done.3, bf16[4,104,768]{2,1,0:T(8,128)(2,1)} %copy-done.18, s32[2]{0:T(128)} %pad_add_fusion.turn_ref), custom_call_target="tpu_custom_call" | custom-call | bytes 3661832 | tf_op jit(solution)/shard_map/pallas_call | solution.py:494
  266.2 2.9 %shard_map.339 = (f32[192,768]{1,0:T(8,128)}, f32[192,768]{1,0:T(8,128)}, f32[192,768]{1,0:T(8,128)}, f32[192,768]{1,0:T(8,128)}, f32[8,768]{1,0:T(8,128)}) custom-call(bf16[4,104,768]{2,1,0:T(8,128)(2,1)} %copy-done.4, bf16[4,104,768]{2,1,0:T(8,128)(2,1)} %copy-done.19, s32[2]{0:T(128)} %pad_add_fusion.turn_ref), custom_call_target="tpu_custom_call" | custom-call | bytes 3661832 | tf_op jit(solution)/shard_map/pallas_call | solution.py:494
  270.2 3.0 %collective-permute-start.52 = (f32[1,768]{1,0:T(1,128)S(1)}, f32[1,768]{1,0:T(1,128)S(1)}, u32[]{:S(2)}, u32[]{:S(2)}) collective-permute-start(f32[1,768]{1,0:T(1,128)S(1)} %add.142), channel_id=1, source_target_pairs={{0,2},{2,0},{1,3},{3,1},{4,6},{6,4},{5,7},{7,5},{8,10},{10,8},{9,1... | collective-permute-start | bytes 9224 | tf_op jit(solution)/shard_map/ppermute | solution.py:519
  (213 shorter events, 58.5 us)
Async XLA Ops:
  2.6 12.3 %collective-permute-start.2 = (bf16[256,768]{1,0:T(8,128)(2,1)}, bf16[256,768]{1,0:T(8,128)(2,1)S(1)}, u32[]{:S(2)}, u32[]{:S(2)}) collective-permute-start(bf16[256,768]{1,0:T(8,128)(2,1)} %shard_map.323.n0), channel_id=1, source_target_pairs={{0,2},{2,0},{1,3},{3,1},{4,6},{6,4},{5,7},{7,5},{8,10},{10,8},{9,1... | collective-permute-start | bytes 1179656 | tf_op jit(solution)/shard_map/ppermute | solution.py:519
  5.5 1.9 collective-permute-start
  14.2 15.6 %collective-permute-start.4 = (bf16[384,768]{1,0:T(8,128)(2,1)S(1)}, bf16[384,768]{1,0:T(8,128)(2,1)}, u32[]{:S(2)}, u32[]{:S(2)}) collective-permute-start(bf16[384,768]{1,0:T(8,128)(2,1)S(1)} %pad_maximum_fusion.3.w0), channel_id=1, source_target_pairs={{0,2},{2,0},{1,3},{3,1},{4,6},{6,4},{5,7},{7,5},{8,10},{10,8},{9,1... | collective-permute-start | bytes 1769480 | tf_op jit(solution)/shard_map/ppermute | solution.py:519
  29.9 2.5 collective-permute-start.5
  29.9 3.2 %collective-permute-start.8 = (bf16[384,768]{1,0:T(8,128)(2,1)S(1)}, bf16[384,768]{1,0:T(8,128)(2,1)}, u32[]{:S(2)}, u32[]{:S(2)}) collective-permute-start(bf16[384,768]{1,0:T(8,128)(2,1)S(1)} %pad_maximum_fusion.3.w0), channel_id=1, source_target_pairs={{0,1},{1,0},{2,3},{3,2},{4,5},{5,4},{6,7},{7,6},{8,9},{9,8},{10,11... | collective-permute-start | bytes 1769480 | tf_op jit(solution)/shard_map/ppermute | solution.py:515
  30.4 3.2 %collective-permute-start.9 = (bf16[384,768]{1,0:T(8,128)(2,1)}, bf16[384,768]{1,0:T(8,128)(2,1)}, u32[]{:S(2)}, u32[]{:S(2)}) collective-permute-start(bf16[384,768]{1,0:T(8,128)(2,1)} %collective-permute-done.4.w2), channel_id=1, source_target_pairs={{0,1},{1,0},{2,3},{3,2},{4,5},{5,4},{6,7},{7,6},{8,9},{9,8},{10,11... | collective-permute-start | bytes 1769480 | tf_op jit(solution)/shard_map/ppermute | solution.py:515
  30.7 9.9 %collective-permute-start.7 = (bf16[192,768]{1,0:T(8,128)(2,1)S(1)}, bf16[192,768]{1,0:T(8,128)(2,1)S(1)}, u32[]{:S(2)}, u32[]{:S(2)}) collective-permute-start(bf16[192,768]{1,0:T(8,128)(2,1)S(1)} %fusion.7), channel_id=1, source_target_pairs={{0,2},{2,0},{1,3},{3,1},{4,6},{6,4},{5,7},{7,5},{8,10},{10,8},{9,1... | collective-permute-start | bytes 884744 | tf_op jit(solution)/shard_map/ppermute | solution.py:519
  32.4 16.2 %collective-permute-start.6 = (bf16[256,768]{1,0:T(8,128)(2,1)S(1)}, bf16[256,768]{1,0:T(8,128)(2,1)S(1)}, u32[]{:S(2)}, u32[]{:S(2)}) collective-permute-start(bf16[256,768]{1,0:T(8,128)(2,1)S(1)} %add_convert_fusion.4), channel_id=1, source_target_pairs={{0,2},{2,0},{1,3},{3,1},{4,6},{6,4},{5,7},{7,5},{8,10},{10,8},{9,1... | collective-permute-start | bytes 1179656 | tf_op jit(solution)/shard_map/ppermute | solution.py:519
  40.6 8.3 %collective-permute-start.11 = (bf16[192,768]{1,0:T(8,128)(2,1)S(1)}, bf16[192,768]{1,0:T(8,128)(2,1)S(1)}, u32[]{:S(2)}, u32[]{:S(2)}) collective-permute-start(bf16[192,768]{1,0:T(8,128)(2,1)S(1)} %collective-permute-done.7.w2), channel_id=1, source_target_pairs={{0,4},{4,0},{8,12},{12,8},{16,20},{20,16},{24,28},{28,24},{1,5},{5... | collective-permute-start | bytes 884744 | tf_op jit(solution)/shard_map/ppermute | solution.py:536
  42.1 8.2 %collective-permute-start.10 = (bf16[384,768]{1,0:T(8,128)(2,1)S(1)}, bf16[384,768]{1,0:T(8,128)(2,1)S(1)}, u32[]{:S(2)}, u32[]{:S(2)}) collective-permute-start(bf16[384,768]{1,0:T(8,128)(2,1)S(1)} %pad_maximum_fusion.w0), channel_id=1, source_target_pairs={{0,1},{1,0},{2,3},{3,2},{4,5},{5,4},{6,7},{7,6},{8,9},{9,8},{10,11... | collective-permute-start | bytes 1769480 | tf_op jit(solution)/shard_map/ppermute | solution.py:515
  42.2 8.1 %collective-permute-start.12 = (bf16[192,768]{1,0:T(8,128)(2,1)S(1)}, bf16[192,768]{1,0:T(8,128)(2,1)}, u32[]{:S(2)}, u32[]{:S(2)}) collective-permute-start(bf16[192,768]{1,0:T(8,128)(2,1)S(1)} %collective-permute-done.7.w2), channel_id=1, source_target_pairs={{0,1},{1,0},{2,3},{3,2},{4,5},{5,4},{6,7},{7,6},{8,9},{9,8},{10,11... | collective-permute-start | bytes 884744 | tf_op jit(solution)/shard_map/ppermute | solution.py:515
  48.9 13.7 %collective-permute-start.17 = (bf16[256,768]{1,0:T(8,128)(2,1)S(1)}, bf16[256,768]{1,0:T(8,128)(2,1)S(1)}, u32[]{:S(2)}, u32[]{:S(2)}) collective-permute-start(bf16[256,768]{1,0:T(8,128)(2,1)S(1)} %copy-done.27), channel_id=1, source_target_pairs={{0,2},{2,0},{1,3},{3,1},{4,6},{6,4},{5,7},{7,5},{8,10},{10,8},{9,1... | collective-permute-start | bytes 1179656 | tf_op jit(solution)/shard_map/ppermute | solution.py:519
  49.6 15.0 %collective-permute-start.16 = (bf16[256,768]{1,0:T(8,128)(2,1)S(1)}, bf16[256,768]{1,0:T(8,128)(2,1)S(1)}, u32[]{:S(2)}, u32[]{:S(2)}) collective-permute-start(bf16[256,768]{1,0:T(8,128)(2,1)S(1)} %copy-done.27), channel_id=1, source_target_pairs={{0,1},{1,0},{2,3},{3,2},{4,5},{5,4},{6,7},{7,6},{8,9},{9,8},{10,11... | collective-permute-start | bytes 1179656 | tf_op jit(solution)/shard_map/ppermute | solution.py:515
  62.6 2.0 collective-permute-start.18
  63.0 8.7 %collective-permute-start.14 = (bf16[256,768]{1,0:T(8,128)(2,1)}, bf16[256,768]{1,0:T(8,128)(2,1)S(1)}, u32[]{:S(2)}, u32[]{:S(2)}) collective-permute-start(bf16[256,768]{1,0:T(8,128)(2,1)} %get-tuple-element.134.g0), channel_id=1, source_target_pairs={{0,1},{1,0},{2,3},{3,2},{4,5},{5,4},{6,7},{7,6},{8,9},{9,8},{10,11... | collective-permute-start | bytes 1179656 | tf_op jit(solution)/shard_map/ppermute | solution.py:515
  63.2 14.9 %collective-permute-start.15 = (bf16[256,768]{1,0:T(8,128)(2,1)}, bf16[256,768]{1,0:T(8,128)(2,1)S(1)}, u32[]{:S(2)}, u32[]{:S(2)}) collective-permute-start(bf16[256,768]{1,0:T(8,128)(2,1)} %get-tuple-element.134.g0), channel_id=1, source_target_pairs={{0,2},{2,0},{1,3},{3,1},{4,6},{6,4},{5,7},{7,5},{8,10},{10,8},{9,1... | collective-permute-start | bytes 1179656 | tf_op jit(solution)/shard_map/ppermute | solution.py:519
  78.0 1.9 collective-permute-start.19
  91.2 12.5 %collective-permute-start.22 = (bf16[256,768]{1,0:T(8,128)(2,1)S(1)}, bf16[256,768]{1,0:T(8,128)(2,1)S(1)}, u32[]{:S(2)}, u32[]{:S(2)}) collective-permute-start(bf16[256,768]{1,0:T(8,128)(2,1)S(1)} %add_convert_fusion.3), channel_id=1, source_target_pairs={{0,2},{2,0},{1,3},{3,1},{4,6},{6,4},{5,7},{7,5},{8,10},{10,8},{9,1... | collective-permute-start | bytes 1179656 | tf_op jit(solution)/shard_map/ppermute | solution.py:519
  102.1 31.4 %collective-permute-start.25 = (bf16[4,192,768]{2,1,0:T(8,128)(2,1)}, bf16[4,192,768]{2,1,0:T(8,128)(2,1)S(1)}, u32[]{:S(2)}, u32[]{:S(2)}) collective-permute-start(bf16[4,192,768]{2,1,0:T(8,128)(2,1)} %get-tuple-element.149), channel_id=1, source_target_pairs={{0,4},{4,0},{8,12},{12,8},{16,20},{20,16},{24,28},{28,24},{1,5},{5... | collective-permute-start | bytes 3538952 | tf_op jit(solution)/shard_map/ppermute | solution.py:536
  122.5 11.0 %collective-permute-start.24 = (bf16[256,768]{1,0:T(8,128)(2,1)}, bf16[256,768]{1,0:T(8,128)(2,1)}, u32[]{:S(2)}, u32[]{:S(2)}) collective-permute-start(bf16[256,768]{1,0:T(8,128)(2,1)} %get-tuple-element.156.u0), channel_id=1, source_target_pairs={{0,2},{2,0},{1,3},{3,1},{4,6},{6,4},{5,7},{7,5},{8,10},{10,8},{9,1... | collective-permute-start | bytes 1179656 | tf_op jit(solution)/shard_map/ppermute | solution.py:519
  134.6 5.6 %collective-permute-start.26 = (bf16[2,8,104,768]{3,2,1,0:T(8,128)(2,1)}, bf16[2,8,104,768]{3,2,1,0:T(8,128)(2,1)S(1)}, u32[]{:S(2)}, u32[]{:S(2)}) collective-permute-start(bf16[2,8,104,768]{3,2,1,0:T(8,128)(2,1)} %get-tuple-element.167), channel_id=1, source_target_pairs={{0,1},{1,0},{2,3},{3,2},{4,5},{5,4},{6,7},{7,6},{8,9},{9,8},{10,11... | collective-permute-start | bytes 7667720 | tf_op jit(solution)/shard_map/ppermute | solution.py:515
  134.6 7.4 %collective-permute-start.23 = (bf16[256,768]{1,0:T(8,128)(2,1)S(1)}, bf16[256,768]{1,0:T(8,128)(2,1)S(1)}, u32[]{:S(2)}, u32[]{:S(2)}) collective-permute-start(bf16[256,768]{1,0:T(8,128)(2,1)S(1)} %copy-done.44), channel_id=1, source_target_pairs={{0,1},{1,0},{2,3},{3,2},{4,5},{5,4},{6,7},{7,6},{8,9},{9,8},{10,11... | collective-permute-start | bytes 1179656 | tf_op jit(solution)/shard_map/ppermute | solution.py:515
  135.1 7.6 %collective-permute-start.27 = (bf16[256,768]{1,0:T(8,128)(2,1)}, bf16[256,768]{1,0:T(8,128)(2,1)S(1)}, u32[]{:S(2)}, u32[]{:S(2)}) collective-permute-start(bf16[256,768]{1,0:T(8,128)(2,1)} %collective-permute-done.24.u2), channel_id=1, source_target_pairs={{0,1},{1,0},{2,3},{3,2},{4,5},{5,4},{6,7},{7,6},{8,9},{9,8},{10,11... | collective-permute-start | bytes 1179656 | tf_op jit(solution)/shard_map/ppermute | solution.py:515
  135.1 22.3 %collective-permute-start.28 = (bf16[2,192,768]{2,1,0:T(8,128)(2,1)}, bf16[2,192,768]{2,1,0:T(8,128)(2,1)}, u32[]{:S(2)}, u32[]{:S(2)}) collective-permute-start(bf16[2,192,768]{2,1,0:T(8,128)(2,1)} %get-tuple-element.222), channel_id=1, source_target_pairs={{0,8},{4,12},{8,0},{12,4},{16,24},{20,28},{24,16},{28,20},{1,9},{5... | collective-permute-start | bytes 1769480 | tf_op jit(solution)/shard_map/ppermute | solution.py:536
  140.5 30.2 %collective-permute-start.33 = (bf16[8,104,768]{2,1,0:T(8,128)(2,1)S(1)}, bf16[8,104,768]{2,1,0:T(8,128)(2,1)S(1)}, u32[]{:S(2)}, u32[]{:S(2)}) collective-permute-start(bf16[8,104,768]{2,1,0:T(8,128)(2,1)S(1)} %fusion.1), channel_id=1, source_target_pairs={{0,2},{2,0},{1,3},{3,1},{4,6},{6,4},{5,7},{7,5},{8,10},{10,8},{9,1... | collective-permute-start | bytes 3833864 | tf_op jit(solution)/shard_map/ppermute | solution.py:519
  159.3 3.1 %collective-permute-start.29 = (bf16[2,256,768]{2,1,0:T(8,128)(2,1)}, bf16[2,256,768]{2,1,0:T(8,128)(2,1)S(1)}, u32[]{:S(2)}, u32[]{:S(2)}) collective-permute-start(bf16[2,256,768]{2,1,0:T(8,128)(2,1)} %get-tuple-element.182), channel_id=1, source_target_pairs={{0,1},{1,0},{2,3},{3,2},{4,5},{5,4},{6,7},{7,6},{8,9},{9,8},{10,11... | collective-permute-start | bytes 2359304 | tf_op jit(solution)/shard_map/ppermute | solution.py:515
  159.3 19.9 %collective-permute-start.32 = (bf16[1,192,768]{2,1,0:T(8,128)(2,1)}, bf16[1,192,768]{2,1,0:T(8,128)(2,1)}, u32[]{:S(2)}, u32[]{:S(2)}) collective-permute-start(bf16[1,192,768]{2,1,0:T(8,128)(2,1)} %add_convert_fusion.11), channel_id=1, source_target_pairs={{0,16},{4,20},{8,24},{12,28},{16,0},{20,4},{24,8},{28,12},{1,17},{... | collective-permute-start | bytes 884744 | tf_op jit(solution)/shard_map/ppermute | solution.py:536
  161.9 18.6 %collective-permute-start.31 = (bf16[4,104,768]{2,1,0:T(8,128)(2,1)}, bf16[4,104,768]{2,1,0:T(8,128)(2,1)}, u32[]{:S(2)}, u32[]{:S(2)}) collective-permute-start(bf16[4,104,768]{2,1,0:T(8,128)(2,1)} %get-tuple-element.181), channel_id=1, source_target_pairs={{0,4},{4,0},{8,12},{12,8},{16,20},{20,16},{24,28},{28,24},{1,5},{5... | collective-permute-start | bytes 1916936 | tf_op jit(solution)/shard_map/ppermute | solution.py:536
  171.3 25.4 %collective-permute-start.36 = (bf16[4,104,768]{2,1,0:T(8,128)(2,1)S(1)}, bf16[4,104,768]{2,1,0:T(8,128)(2,1)S(1)}, u32[]{:S(2)}, u32[]{:S(2)}) collective-permute-start(bf16[4,104,768]{2,1,0:T(8,128)(2,1)S(1)} %slice.165), channel_id=1, source_target_pairs={{0,4},{4,0},{8,12},{12,8},{16,20},{20,16},{24,28},{28,24},{1,5},{5... | collective-permute-start | bytes 1916936 | tf_op jit(solution)/shard_map/ppermute | solution.py:536
  181.7 14.3 %collective-permute-start.34 = (bf16[2,104,768]{2,1,0:T(8,128)(2,1)S(1)}, bf16[2,104,768]{2,1,0:T(8,128)(2,1)S(1)}, u32[]{:S(2)}, u32[]{:S(2)}) collective-permute-start(bf16[2,104,768]{2,1,0:T(8,128)(2,1)S(1)} %get-tuple-element.225), channel_id=1, source_target_pairs={{0,8},{4,12},{8,0},{12,4},{16,24},{20,28},{24,16},{28,20},{1,9},{5... | collective-permute-start | bytes 958472 | tf_op jit(solution)/shard_map/ppermute | solution.py:536
  183.4 30.8 %collective-permute-start.30 = (bf16[256,768]{1,0:T(8,128)(2,1)S(1)}, bf16[256,768]{1,0:T(8,128)(2,1)S(1)}, u32[]{:S(2)}, u32[]{:S(2)}) collective-permute-start(bf16[256,768]{1,0:T(8,128)(2,1)S(1)} %copy-done.34), channel_id=1, source_target_pairs={{0,2},{2,0},{1,3},{3,1},{4,6},{6,4},{5,7},{7,5},{8,10},{10,8},{9,1... | collective-permute-start | bytes 1179656 | tf_op jit(solution)/shard_map/ppermute | solution.py:519
  184.7 18.7 %collective-permute-start.42 = (bf16[1,192,768]{2,1,0:T(8,128)(2,1)S(1)}, bf16[1,192,768]{2,1,0:T(8,128)(2,1)S(1)}, u32[]{:S(2)}, u32[]{:S(2)}) collective-permute-start(bf16[1,192,768]{2,1,0:T(8,128)(2,1)S(1)} %add_convert_fusion.9), channel_id=1, source_target_pairs={{0,16},{4,20},{8,24},{12,28},{16,0},{20,4},{24,8},{28,12},{1,17},{... | collective-permute-start | bytes 884744 | tf_op jit(solution)/shard_map/ppermute | solution.py:536
  196.0 10.4 %collective-permute-start.35 = (bf16[1,104,768]{2,1,0:T(8,128)(2,1)S(1)}, bf16[1,104,768]{2,1,0:T(8,128)(2,1)S(1)}, u32[]{:S(2)}, u32[]{:S(2)}) collective-permute-start(bf16[1,104,768]{2,1,0:T(8,128)(2,1)S(1)} %add_convert_fusion.16), channel_id=1, source_target_pairs={{0,16},{4,20},{8,24},{12,28},{16,0},{20,4},{24,8},{28,12},{1,17},{... | collective-permute-start | bytes 479240 | tf_op jit(solution)/shard_map/ppermute | solution.py:536
  196.8 12.3 %collective-permute-start.37 = (bf16[2,104,768]{2,1,0:T(8,128)(2,1)S(1)}, bf16[2,104,768]{2,1,0:T(8,128)(2,1)S(1)}, u32[]{:S(2)}, u32[]{:S(2)}) collective-permute-start(bf16[2,104,768]{2,1,0:T(8,128)(2,1)S(1)} %get-tuple-element.224), channel_id=1, source_target_pairs={{0,8},{4,12},{8,0},{12,4},{16,24},{20,28},{24,16},{28,20},{1,9},{5... | collective-permute-start | bytes 958472 | tf_op jit(solution)/shard_map/ppermute | solution.py:536
  206.5 13.0 %collective-permute-start.40 = (bf16[1,104,768]{2,1,0:T(8,128)(2,1)S(1)}, bf16[1,104,768]{2,1,0:T(8,128)(2,1)S(1)}, u32[]{:S(2)}, u32[]{:S(2)}) collective-permute-start(bf16[1,104,768]{2,1,0:T(8,128)(2,1)S(1)} %add_convert_fusion.15), channel_id=1, source_target_pairs={{0,16},{4,20},{8,24},{12,28},{16,0},{20,4},{24,8},{28,12},{1,17},{... | collective-permute-start | bytes 479240 | tf_op jit(solution)/shard_map/ppermute | solution.py:536
  209.1 13.6 %collective-permute-start.44 = (bf16[1,104,768]{2,1,0:T(8,128)(2,1)S(1)}, bf16[1,104,768]{2,1,0:T(8,128)(2,1)S(1)}, u32[]{:S(2)}, u32[]{:S(2)}) collective-permute-start(bf16[1,104,768]{2,1,0:T(8,128)(2,1)S(1)} %add_convert_fusion.14), channel_id=1, source_target_pairs={{0,16},{4,20},{8,24},{12,28},{16,0},{20,4},{24,8},{28,12},{1,17},{... | collective-permute-start | bytes 479240 | tf_op jit(solution)/shard_map/ppermute | solution.py:536
  210.5 14.9 %collective-permute-start.45 = (bf16[2,96,768]{2,1,0:T(8,128)(2,1)S(1)}, bf16[2,96,768]{2,1,0:T(8,128)(2,1)S(1)}, u32[]{:S(2)}, u32[]{:S(2)}) collective-permute-start(bf16[2,96,768]{2,1,0:T(8,128)(2,1)S(1)} %get-tuple-element.227), channel_id=1, source_target_pairs={{0,8},{4,12},{8,0},{12,4},{16,24},{20,28},{24,16},{28,20},{1,9},{5... | collective-permute-start | bytes 884744 | tf_op jit(solution)/shard_map/ppermute | solution.py:536
  212.6 12.9 %collective-permute-start.43 = (bf16[2,96,768]{2,1,0:T(8,128)(2,1)S(1)}, bf16[2,96,768]{2,1,0:T(8,128)(2,1)S(1)}, u32[]{:S(2)}, u32[]{:S(2)}) collective-permute-start(bf16[2,96,768]{2,1,0:T(8,128)(2,1)S(1)} %get-tuple-element.228), channel_id=1, source_target_pairs={{0,4},{4,0},{8,12},{12,8},{16,20},{20,16},{24,28},{28,24},{1,5},{5... | collective-permute-start | bytes 884744 | tf_op jit(solution)/shard_map/ppermute | solution.py:536
  219.5 14.8 %collective-permute-start.41 = (bf16[2,104,768]{2,1,0:T(8,128)(2,1)S(1)}, bf16[2,104,768]{2,1,0:T(8,128)(2,1)S(1)}, u32[]{:S(2)}, u32[]{:S(2)}) collective-permute-start(bf16[2,104,768]{2,1,0:T(8,128)(2,1)S(1)} %pad_maximum_fusion.6), channel_id=1, source_target_pairs={{0,8},{4,12},{8,0},{12,4},{16,24},{20,28},{24,16},{28,20},{1,9},{5... | collective-permute-start | bytes 958472 | tf_op jit(solution)/shard_map/ppermute | solution.py:536
  219.6 27.1 %collective-permute-start.38 = (bf16[2,256,768]{2,1,0:T(8,128)(2,1)S(1)}, bf16[2,256,768]{2,1,0:T(8,128)(2,1)S(1)}, u32[]{:S(2)}, u32[]{:S(2)}) collective-permute-start(bf16[2,256,768]{2,1,0:T(8,128)(2,1)S(1)} %copy-done.40), channel_id=1, source_target_pairs={{0,1},{1,0},{2,3},{3,2},{4,5},{5,4},{6,7},{7,6},{8,9},{9,8},{10,11... | collective-permute-start | bytes 2359304 | tf_op jit(solution)/shard_map/ppermute | solution.py:515
  222.7 11.7 %collective-permute-start.47 = (bf16[1,104,768]{2,1,0:T(8,128)(2,1)S(1)}, bf16[1,104,768]{2,1,0:T(8,128)(2,1)S(1)}, u32[]{:S(2)}, u32[]{:S(2)}) collective-permute-start(bf16[1,104,768]{2,1,0:T(8,128)(2,1)S(1)} %add_convert_fusion.12), channel_id=1, source_target_pairs={{0,16},{4,20},{8,24},{12,28},{16,0},{20,4},{24,8},{28,12},{1,17},{... | collective-permute-start | bytes 479240 | tf_op jit(solution)/shard_map/ppermute | solution.py:536
  225.5 14.8 %collective-permute-start.49 = (bf16[4,96,768]{2,1,0:T(8,128)(2,1)S(1)}, bf16[4,96,768]{2,1,0:T(8,128)(2,1)S(1)}, u32[]{:S(2)}, u32[]{:S(2)}) collective-permute-start(bf16[4,96,768]{2,1,0:T(8,128)(2,1)S(1)} %pad_maximum_fusion.5.low_ref), channel_id=1, source_target_pairs={{0,4},{4,0},{8,12},{12,8},{16,20},{20,16},{24,28},{28,24},{1,5},{5... | collective-permute-start | bytes 1769480 | tf_op jit(solution)/shard_map/ppermute | solution.py:536
  234.5 10.5 %collective-permute-start.48 = (bf16[2,104,768]{2,1,0:T(8,128)(2,1)S(1)}, bf16[2,104,768]{2,1,0:T(8,128)(2,1)S(1)}, u32[]{:S(2)}, u32[]{:S(2)}) collective-permute-start(bf16[2,104,768]{2,1,0:T(8,128)(2,1)S(1)} %pad_maximum_fusion.7), channel_id=1, source_target_pairs={{0,8},{4,12},{8,0},{12,4},{16,24},{20,28},{24,16},{28,20},{1,9},{5... | collective-permute-start | bytes 958472 | tf_op jit(solution)/shard_map/ppermute | solution.py:536
  234.6 24.2 %collective-permute-start.46 = (bf16[4,104,768]{2,1,0:T(8,128)(2,1)S(1)}, bf16[4,104,768]{2,1,0:T(8,128)(2,1)S(1)}, u32[]{:S(2)}, u32[]{:S(2)}) collective-permute-start(bf16[4,104,768]{2,1,0:T(8,128)(2,1)S(1)} %pad_maximum_fusion.1.low_ref), channel_id=1, source_target_pairs={{0,4},{4,0},{8,12},{12,8},{16,20},{20,16},{24,28},{28,24},{1,5},{5... | collective-permute-start | bytes 1916936 | tf_op jit(solution)/shard_map/ppermute | solution.py:536
  236.2 18.9 %collective-permute-start.53 = (bf16[4,96,768]{2,1,0:T(8,128)(2,1)S(1)}, bf16[4,96,768]{2,1,0:T(8,128)(2,1)S(1)}, u32[]{:S(2)}, u32[]{:S(2)}) collective-permute-start(bf16[4,96,768]{2,1,0:T(8,128)(2,1)S(1)} %pad_maximum_fusion.4.low_ref), channel_id=1, source_target_pairs={{0,8},{4,12},{8,0},{12,4},{16,24},{20,28},{24,16},{28,20},{1,9},{5... | collective-permute-start | bytes 1769480 | tf_op jit(solution)/shard_map/ppermute | solution.py:536
  245.1 20.3 %collective-permute-start.50 = (bf16[4,104,768]{2,1,0:T(8,128)(2,1)S(1)}, bf16[4,104,768]{2,1,0:T(8,128)(2,1)S(1)}, u32[]{:S(2)}, u32[]{:S(2)}) collective-permute-start(bf16[4,104,768]{2,1,0:T(8,128)(2,1)S(1)} %pad_maximum_fusion.2.low_ref), channel_id=1, source_target_pairs={{0,4},{4,0},{8,12},{12,8},{16,20},{20,16},{24,28},{28,24},{1,5},{5... | collective-permute-start | bytes 1916936 | tf_op jit(solution)/shard_map/ppermute | solution.py:536
  246.8 22.3 %collective-permute-start.39 = (bf16[256,768]{1,0:T(8,128)(2,1)S(1)}, bf16[256,768]{1,0:T(8,128)(2,1)S(1)}, u32[]{:S(2)}, u32[]{:S(2)}) collective-permute-start(bf16[256,768]{1,0:T(8,128)(2,1)S(1)} %fusion.2), channel_id=1, source_target_pairs={{0,2},{2,0},{1,3},{3,1},{4,6},{6,4},{5,7},{7,5},{8,10},{10,8},{9,1... | collective-permute-start | bytes 1179656 | tf_op jit(solution)/shard_map/ppermute | solution.py:519
  270.2 4.6 %collective-permute-start.52 = (f32[1,768]{1,0:T(1,128)S(1)}, f32[1,768]{1,0:T(1,128)S(1)}, u32[]{:S(2)}, u32[]{:S(2)}) collective-permute-start(f32[1,768]{1,0:T(1,128)S(1)} %add.142), channel_id=1, source_target_pairs={{0,2},{2,0},{1,3},{3,1},{4,6},{6,4},{5,7},{7,5},{8,10},{10,8},{9,1... | collective-permute-start | bytes 9224 | tf_op jit(solution)/shard_map/ppermute | solution.py:519
  (55 other events, 321.9 us)
where the time goes:
time: 276 us; the launch traced here: 275 us
  Pallas kernels  120 us (43%)
  waiting for transfers between devices  76.3 us (28%)
  starting transfers between devices  48.7 us (18%)
  local copies, waits for them, and re-layouts  14.6 us (5%)
  other arithmetic  12.6 us (5%)
    pallas_call x18, Pallas kernels, call(): pl.pallas_call(kernel, out_shape=[jax.ShapeDtypeStruct(s, t) for s, t in...  120 us
    ppermute x21, waiting for transfers between devices, swap_dp(): lax.ppermute(a, 'dp', [(i, i ^ 1 << bit) for i in range(lax.axis_size('dp...  40.6 us
    ppermute x21, starting transfers between devices, swap_dp(): lax.ppermute(a, 'dp', [(i, i ^ 1 << bit) for i in range(lax.axis_size('dp...  27.6 us
    ppermute x12, waiting for transfers between devices, swap_chip(): return lax.ppermute(a, 'mp', [(0, 2), (2, 0), (1, 3), (3, 1)])  22 us
    ppermute x12, starting transfers between devices, swap_chip(): return lax.ppermute(a, 'mp', [(0, 2), (2, 0), (1, 3), (3, 1)])  17.8 us
    ppermute x21, waiting for transfers between devices, swap_core(): return lax.ppermute(a, 'mp', [(0, 1), (1, 0), (2, 3), (3, 2)])  13.7 us
    unnamed x98, local copies, waits for them, and re-layouts  11.6 us
    convert_element_type x9, other arithmetic, plus(): return (a.astype(f32) + b.astype(f32)).astype(bf16)  5.79 us
  transfers between devices with their start and end apart: 54, of which 32 were waited for; matrix products, arithmetic and copies ran while one was open for 5% of the time, Pallas kernels for 41%

commit v1 on v0

--- a/solution.py
+++ b/solution.py
@@ -835,7 +835,7 @@
         if feed or name == "one":
             chains.tokens = (grads[name][-1],)
     extra = grads["two"][-1]
-    gain_one = after(extra[:1], *chains.tokens)
+    gain_one = after(extra[:1], chains.last["one"][1])
     gain_one = gain_one + swap_core(gain_one)
     gain_one = gain_one + swap_chip(gain_one)
     layer_out = (after_cross + out_own + got_out[0].astype(f32) + out_far.astype(f32)).astype(bf16)

time: 276 us -> 275 us (level)
  transfers between devices with their start and end apart: 54 -> 54, of which waited for: 32 -> 31; matrix products, arithmetic and copies ran while one was open for 5% -> 5% of each run, Pallas kernels for 41% -> 41%
where the time goes in v1:
time: 275 us
  Pallas kernels  120 us (44%)
  waiting for transfers between devices  76.1 us (28%)
  starting transfers between devices  48.8 us (18%)
  local copies, waits for them, and re-layouts  13.7 us (5%)
  other arithmetic  12.6 us (5%)
    pallas_call x18, Pallas kernels, call(): pl.pallas_call(kernel, out_shape=[jax.ShapeDtypeStruct(s, t) for s, t in...  120 us
    ppermute x21, waiting for transfers between devices, swap_dp(): lax.ppermute(a, 'dp', [(i, i ^ 1 << bit) for i in range(lax.axis_size('dp...  40.5 us
    ppermute x21, starting transfers between devices, swap_dp(): lax.ppermute(a, 'dp', [(i, i ^ 1 << bit) for i in range(lax.axis_size('dp...  27.6 us
    ppermute x12, waiting for transfers between devices, swap_chip(): return lax.ppermute(a, 'mp', [(0, 2), (2, 0), (1, 3), (3, 1)])  22.1 us
    ppermute x12, starting transfers between devices, swap_chip(): return lax.ppermute(a, 'mp', [(0, 2), (2, 0), (1, 3), (3, 1)])  17.9 us
    ppermute x21, waiting for transfers between devices, swap_core(): return lax.ppermute(a, 'mp', [(0, 1), (1, 0), (2, 3), (3, 2)])  13.6 us
    unnamed x98, local copies, waits for them, and re-layouts  10.8 us
    convert_element_type x9, other arithmetic, plus(): return (a.astype(f32) + b.astype(f32)).astype(bf16)  5.78 us
  transfers between devices with their start and end apart: 54, of which 31 were waited for; matrix products, arithmetic and copies ran while one was open for 5% of the time, Pallas kernels for 41%

profile of v1, /device:TPU:0, one launch (start us, length us, event | category | flops | bytes accessed | tf_op | source)
XLA Modules:
  0.0 274.5 jit_solution(17467992010420181308)
XLA Ops:
  0.7 1.9 shard_map.323.n0
  2.6 2.9 %collective-permute-start.2 = (bf16[256,768]{1,0:T(8,128)(2,1)}, bf16[256,768]{1,0:T(8,128)(2,1)S(1)}, u32[]{:S(2)}, u32[]{:S(2)}) collective-permute-start(bf16[256,768]{1,0:T(8,128)(2,1)} %shard_map.323.n0), channel_id=1, source_target_pairs={{0,2},{2,0},{1,3},{3,1},{4,6},{6,4},{5,7},{7,5},{8,10},{10,8},{9,1... | collective-permute-start | bytes 1179656 | tf_op jit(solution)/shard_map/ppermute | solution.py:519
  8.2 5.6 %shard_map.324 = (bf16[512,192]{1,0:T(8,128)(2,1)}, bf16[512,192]{1,0:T(8,128)(2,1)}, bf16[512,192]{1,0:T(8,128)(2,1)}, bf16[512,192]{1,0:T(8,128)(2,1)}, f32[256,768]{1,0:T(8,128)}, /*index=5*/bf16[256,768]{1,0:T(8,128)(2,1)}) custom-call(bf16[256,768]{1,0:T(8,128)(2,1)} %shard_map.323.n0, bf16[256,768]{1,0:T(8,128)(2,1)} %copy-done.42, ...), custom_call_target="tpu_custom_call" | custom-call | flops 603979776 | bytes 3933732 | tf_op jit(solution)/shard_map/pallas_call | solution.py:494
  18.3 5.6 %shard_map.325 = (bf16[512,192]{1,0:T(8,128)(2,1)}, bf16[512,192]{1,0:T(8,128)(2,1)}, bf16[512,192]{1,0:T(8,128)(2,1)}, bf16[512,192]{1,0:T(8,128)(2,1)}, f32[256,768]{1,0:T(8,128)}, /*index=5*/bf16[256,768]{1,0:T(8,128)(2,1)}) custom-call(bf16[256,768]{1,0:T(8,128)(2,1)} %copy-done.41, bf16[256,768]{1,0:T(8,128)(2,1)} %copy-done.43, ...), custom_call_target="tpu_custom_call" | custom-call | flops 603979776 | bytes 3933732 | tf_op jit(solution)/shard_map/pallas_call | solution.py:494
  23.9 6.0 %collective-permute-done.4.w2 = bf16[384,768]{1,0:T(8,128)(2,1)} collective-permute-done((bf16[384,768]{1,0:T(8,128)(2,1)S(1)}, bf16[384,768]{1,0:T(8,128)(2,1)}, u32[]{:S(2)}, u32[]{:S(2)}) %collective-permute-start.4) | collective-permute-done | bytes 589856 | tf_op jit(solution)/shard_map/ppermute | solution.py:519
  33.6 6.2 %shard_map.326 = (bf16[1024,768]{1,0:T(8,128)(2,1)}, bf16[1024,768]{1,0:T(8,128)(2,1)}) custom-call(bf16[1024,768]{1,0:T(8,128)(2,1)} %mem_ref.2, bf16[384,768]{1,0:T(8,128)(2,1)} %copy-done.22, bf16[384,768]{1,0:T(8,128)(2,1)} %collective-permute-done.8.w1, bf16[384,768]{1,0:T(8,128)(2,1)} %collective-permute-done.4.w2, ...), custom_call_target="tpu_custom_call" | custom-call | flops 2415919104 | bytes 7077888 | tf_op jit(solution)/shard_map/pallas_call | solution.py:494
  42.7 5.9 %collective-permute-done.6.far_ref = bf16[256,768]{1,0:T(8,128)(2,1)S(1)} collective-permute-done((bf16[256,768]{1,0:T(8,128)(2,1)S(1)}, bf16[256,768]{1,0:T(8,128)(2,1)S(1)}, u32[]{:S(2)}, u32[]{:S(2)}) %collective-permute-start.6) | collective-permute-done | bytes 393248 | tf_op jit(solution)/shard_map/ppermute | solution.py:519
  51.2 11.4 %shard_map.327 = (f32[256,768]{1,0:T(8,128)}, bf16[256,768]{1,0:T(8,128)(2,1)}, bf16[256,768]{1,0:T(8,128)(2,1)}, bf16[256,768]{1,0:T(8,128)(2,1)}, f32[256,768]{1,0:T(8,128)}, /*index=5*/bf16[256,768]{1,0:T(8,128)(2,1)}) custom-call(bf16[256,768]{1,0:T(8,128)(2,1)} %x_ref.5, f32[256,768]{1,0:T(8,128)} %get-tuple-element.118.own_ref, ...), custom_call_target="tpu_custom_call" | custom-call | flops 1811939328 | bytes 10623020 | tf_op jit(solution)/shard_map/pallas_call | solution.py:494
  66.1 5.6 %shard_map.328.hidden_ref = f32[1024,768]{1,0:T(8,128)} custom-call(bf16[256,768]{1,0:T(8,128)(2,1)} %cot_ref.1, bf16[256,768]{1,0:T(8,128)(2,1)} %copy-done.29, bf16[256,768]{1,0:T(8,128)(2,1)} %copy-done.28, bf16[256,768]{1,0:T(8,128)(2,1)} %copy-done.30, bf16[768,768]{1,0:T(8,128)(2,1)} %out_ref.3), custom_call_target="tpu_custom_call" | custom-call | flops 1207959552 | bytes 5898240 | tf_op jit(solution)/shard_map/pallas_call | solution.py:494
  72.5 5.5 %shard_map.329 = (f32[256,768]{1,0:T(8,128)}, bf16[256,768]{1,0:T(8,128)(2,1)}, bf16[512,768]{1,0:T(8,128)(2,1)}, bf16[512,768]{1,0:T(8,128)(2,1)}) custom-call(bf16[256,768]{1,0:T(8,128)(2,1)} %get-tuple-element.134.g0, bf16[256,768]{1,0:T(8,128)(2,1)} %copy-done.31, f32[1024,768]{1,0:T(8,128)} %shard_map.328.hidden_ref, bf16[768,768]{1,0:T(8,128)(2,1)} %in_ref.3), custom_call_target="tpu_custom_call" | custom-call | flops 1207959552 | bytes 7864320 | tf_op jit(solution)/shard_map/pallas_call | solution.py:494
  78.1 1.9 collective-permute-done.19.near_ref
  80.1 1.6 collective-permute-done.20.g1.g3
  82.4 5.6 %shard_map.330 = (f32[256,768]{1,0:T(8,128)}, bf16[256,768]{1,0:T(8,128)(2,1)}, bf16[512,768]{1,0:T(8,128)(2,1)}, bf16[512,768]{1,0:T(8,128)(2,1)}) custom-call(bf16[256,768]{1,0:T(8,128)(2,1)} %copy-done.32, bf16[256,768]{1,0:T(8,128)(2,1)} %copy-done.33, f32[1024,768]{1,0:T(8,128)} %shard_map.328.hidden_ref, bf16[768,768]{1,0:T(8,128)(2,1)} %in_ref.3), custom_call_target="tpu_custom_call" | custom-call | flops 1207959552 | bytes 7864320 | tf_op jit(solution)/shard_map/pallas_call | solution.py:494
  88.2 1.8 collective-permute-done.21
  91.9 10.2 %shard_map.331 = (f32[256,768]{1,0:T(8,128)}, f32[256,768]{1,0:T(8,128)}, bf16[2,256,768]{2,1,0:T(8,128)(2,1)}, bf16[4,192,768]{2,1,0:T(8,128)(2,1)}, bf16[4,192,768]{2,1,0:T(8,128)(2,1)}) custom-call(bf16[256,768]{1,0:T(8,128)(2,1)} %get-tuple-element.134.g0, bf16[256,768]{1,0:T(8,128)(2,1)} %copy-done.31, bf16[256,768]{1,0:T(8,128)(2,1)} %copy-done.32, ...), custom_call_target="tpu_custom_call" | custom-call | flops 3623878656 | bytes 12189704 | tf_op jit(solution)/shard_map/pallas_call | solution.py:494
  102.1 1.6 collective-permute-start.25
  104.4 18.1 %shard_map.332 = (f32[256,768]{1,0:T(8,128)}, bf16[256,768]{1,0:T(8,128)(2,1)}, bf16[768,1024]{1,0:T(8,128)(2,1)}, bf16[768,1024]{1,0:T(8,128)(2,1)}, f32[2,768]...) custom-call(f32[256,768]{1,0:T(8,128)} %get-tuple-element.148.own_ref, ...), custom_call_target="tpu_custom_call" | custom-call | flops 4831838208 | bytes 16920620 | tf_op jit(solution)/shard_map/pallas_call | solution.py:494
  124.0 8.0 %shard_map.333 = (bf16[2,8,104,768]{3,2,1,0:T(8,128)(2,1)}, bf16[2,8,104,768]{3,2,1,0:T(8,128)(2,1)}) custom-call(bf16[768,1024]{1,0:T(8,128)(2,1)} %get-tuple-element.186.dk_ref, bf16[768,1024]{1,0:T(8,128)(2,1)} %get-tuple-element.158.dv_ref, bf16[1024,768]{1,0:T(8,128)(2,1)} %mem_ref.2, bf16[2,8,48,768]{3,2,1,0:T(8,128)(2,1)} %get-tuple-element.159.keep_in, ...), custom_call_target="tpu_custom_call" | custom-call | flops 2415919104 | bytes 12195848 | tf_op jit(solution)/shard_map/pallas_call | solution.py:494
  135.1 1.6 collective-permute-start.28
  136.7 3.5 %collective-permute-done.26 = bf16[2,8,104,768]{3,2,1,0:T(8,128)(2,1)S(1)} collective-permute-done((bf16[2,8,104,768]{3,2,1,0:T(8,128)(2,1)}, bf16[2,8,104,768]{3,2,1,0:T(8,128)(2,1)S(1)}, u32[]{:S(2)}, u32[]{:S(2)}) %collective-permute-start.26) | collective-permute-done | bytes 2555936 | tf_op jit(solution)/shard_map/ppermute | solution.py:515
  143.5 13.9 %shard_map.334 = (bf16[4,104,768]{2,1,0:T(8,128)(2,1)}, bf16[4,104,768]{2,1,0:T(8,128)(2,1)}, f32[256,768]{1,0:T(8,128)}, f32[256,768]{1,0:T(8,128)}, bf16[2,256,768]{2,1,0:T(8,128)(2,1)}) custom-call(bf16[256,768]{1,0:T(8,128)(2,1)} %get-tuple-element.156.u0, bf16[256,768]{1,0:T(8,128)(2,1)} %copy-done.47, bf16[256,768]{1,0:T(8,128)(2,1)} %collective-permute-done.24.u2, ...), custom_call_target="tpu_custom_call" | custom-call | flops 3019898880 | bytes 9540140 | tf_op jit(solution)/shard_map/pallas_call | solution.py:494
  157.4 1.8 add_convert_fusion.11
  159.3 2.6 collective-permute-start.32
  163.4 7.3 %collective-permute-done.33 = bf16[8,104,768]{2,1,0:T(8,128)(2,1)S(1)} collective-permute-done((bf16[8,104,768]{2,1,0:T(8,128)(2,1)S(1)}, bf16[8,104,768]{2,1,0:T(8,128)(2,1)S(1)}, u32[]{:S(2)}, u32[]{:S(2)}) %collective-permute-start.33) | collective-permute-done | bytes 1277984 | tf_op jit(solution)/shard_map/ppermute | solution.py:519
  171.8 7.3 %shard_map.335 = f32[1024,768]{1,0:T(8,128)} custom-call(bf16[768,1024]{1,0:T(8,128)(2,1)} %get-tuple-element.186.dk_ref, bf16[768,1024]{1,0:T(8,128)(2,1)} %get-tuple-element.158.dv_ref, bf16[384,768]{1,0:T(8,128)(2,1)} %copy-done.22, bf16[384,768]{1,0:T(8,128)(2,1)} %collective-permute-done.8.w1, bf16[384,768]{1,0:T(8,128)(2,1)} %collective-permute-done.4.w2, ...), custom_call_target="tpu_custom_call" | custom-call | flops 2415919104 | bytes 8650752 | tf_op jit(solution)/shard_map/pallas_call | solution.py:494
  181.7 1.6 collective-permute-start.34
  184.7 2.6 collective-permute-start.42
  187.3 8.7 %collective-permute-done.34 = bf16[2,104,768]{2,1,0:T(8,128)(2,1)S(1)} collective-permute-done((bf16[2,104,768]{2,1,0:T(8,128)(2,1)S(1)}, bf16[2,104,768]{2,1,0:T(8,128)(2,1)S(1)}, u32[]{:S(2)}, u32[]{:S(2)}) %collective-permute-start.34) | collective-permute-done | bytes 319520 | tf_op jit(solution)/shard_map/ppermute | solution.py:536
  196.8 2.5 collective-permute-start.37
  200.1 3.3 %collective-permute-done.42 = bf16[1,192,768]{2,1,0:T(8,128)(2,1)S(1)} collective-permute-done((bf16[1,192,768]{2,1,0:T(8,128)(2,1)S(1)}, bf16[1,192,768]{2,1,0:T(8,128)(2,1)S(1)}, u32[]{:S(2)}, u32[]{:S(2)}) %collective-permute-start.42) | collective-permute-done | bytes 294944 | tf_op jit(solution)/shard_map/ppermute | solution.py:536
  203.4 3.0 %collective-permute-done.35 = bf16[1,104,768]{2,1,0:T(8,128)(2,1)S(1)} collective-permute-done((bf16[1,104,768]{2,1,0:T(8,128)(2,1)S(1)}, bf16[1,104,768]{2,1,0:T(8,128)(2,1)S(1)}, u32[]{:S(2)}, u32[]{:S(2)}) %collective-permute-start.35) | collective-permute-done | bytes 159776 | tf_op jit(solution)/shard_map/ppermute | solution.py:536
  206.6 2.5 collective-permute-done.37
  210.5 2.0 collective-permute-start.45
  214.9 3.1 %shard_map.336 = f32[256,768]{1,0:T(8,128)} custom-call(f32[256,768]{1,0:T(8,128)} %get-tuple-element.155.grad_one_ref, f32[256,768]{1,0:T(8,128)} %get-tuple-element.177.own_ref, bf16[256,768]{1,0:T(8,128)(2,1)} %slice_bitcast_fusion.3.near_ref, bf16[256,768]{1,0:T(8,128)(2,1)} %copy-done.35, bf16[256,768]{1,0:T(8,128)(2,1)} %x_ref.5, f32[768]{0:T(1024)} %gain_ref.5), custom_call_target="tpu_custom_call" | custom-call | bytes 3542016 | tf_op jit(solution)/shard_map/pallas_call | solution.py:494
  219.7 3.0 %collective-permute-done.44 = bf16[1,104,768]{2,1,0:T(8,128)(2,1)S(1)} collective-permute-done((bf16[1,104,768]{2,1,0:T(8,128)(2,1)S(1)}, bf16[1,104,768]{2,1,0:T(8,128)(2,1)S(1)}, u32[]{:S(2)}, u32[]{:S(2)}) %collective-permute-start.44) | collective-permute-done | bytes 159776 | tf_op jit(solution)/shard_map/ppermute | solution.py:536
  222.8 2.7 collective-permute-done.45
  225.5 1.6 collective-permute-start.49
  227.2 7.2 %collective-permute-done.41 = bf16[2,104,768]{2,1,0:T(8,128)(2,1)S(1)} collective-permute-done((bf16[2,104,768]{2,1,0:T(8,128)(2,1)S(1)}, bf16[2,104,768]{2,1,0:T(8,128)(2,1)S(1)}, u32[]{:S(2)}, u32[]{:S(2)}) %collective-permute-start.41) | collective-permute-done | bytes 319520 | tf_op jit(solution)/shard_map/ppermute | solution.py:536
  234.6 1.6 collective-permute-start.46
  236.2 1.9 collective-permute-start.53
  238.1 2.2 collective-permute-done.49.high_ref
  241.1 2.9 %shard_map.337 = f32[768,768]{1,0:T(8,128)} custom-call(bf16[4,96,768]{2,1,0:T(8,128)(2,1)} %copy-done.7, bf16[4,96,768]{2,1,0:T(8,128)(2,1)} %copy-done.24, s32[2]{0:T(128)} %pad_add_fusion.turn_ref), custom_call_target="tpu_custom_call" | custom-call | bytes 3538952 | tf_op jit(solution)/shard_map/pallas_call | solution.py:494
  246.8 3.8 %collective-permute-start.39 = (bf16[256,768]{1,0:T(8,128)(2,1)S(1)}, bf16[256,768]{1,0:T(8,128)(2,1)S(1)}, u32[]{:S(2)}, u32[]{:S(2)}) collective-permute-start(bf16[256,768]{1,0:T(8,128)(2,1)S(1)} %fusion.2), channel_id=1, source_target_pairs={{0,2},{2,0},{1,3},{3,1},{4,6},{6,4},{5,7},{7,5},{8,10},{10,8},{9,1... | collective-permute-start | bytes 1179656 | tf_op jit(solution)/shard_map/ppermute | solution.py:519
  250.5 4.5 %collective-permute-done.53.high_ref = bf16[4,96,768]{2,1,0:T(8,128)(2,1)S(1)} collective-permute-done((bf16[4,96,768]{2,1,0:T(8,128)(2,1)S(1)}, bf16[4,96,768]{2,1,0:T(8,128)(2,1)S(1)}, u32[]{:S(2)}, u32[]{:S(2)}) %collective-permute-start.53) | collective-permute-done | bytes 589856 | tf_op jit(solution)/shard_map/ppermute | solution.py:536
  255.9 3.0 %shard_map.340 = f32[768,768]{1,0:T(8,128)} custom-call(bf16[4,96,768]{2,1,0:T(8,128)(2,1)} %copy-done.6, bf16[4,96,768]{2,1,0:T(8,128)(2,1)} %copy-done.23, s32[2]{0:T(128)} %pad_add_fusion.turn_ref), custom_call_target="tpu_custom_call" | custom-call | bytes 3538952 | tf_op jit(solution)/shard_map/pallas_call | solution.py:494
  259.7 2.9 %shard_map.338 = (f32[192,768]{1,0:T(8,128)}, f32[192,768]{1,0:T(8,128)}, f32[192,768]{1,0:T(8,128)}, f32[192,768]{1,0:T(8,128)}, f32[8,768]{1,0:T(8,128)}) custom-call(bf16[4,104,768]{2,1,0:T(8,128)(2,1)} %copy-done.3, bf16[4,104,768]{2,1,0:T(8,128)(2,1)} %copy-done.19, s32[2]{0:T(128)} %pad_add_fusion.turn_ref), custom_call_target="tpu_custom_call" | custom-call | bytes 3661832 | tf_op jit(solution)/shard_map/pallas_call | solution.py:494
  266.4 2.9 %shard_map.339 = (f32[192,768]{1,0:T(8,128)}, f32[192,768]{1,0:T(8,128)}, f32[192,768]{1,0:T(8,128)}, f32[192,768]{1,0:T(8,128)}, f32[8,768]{1,0:T(8,128)}) custom-call(bf16[4,104,768]{2,1,0:T(8,128)(2,1)} %copy-done.4, bf16[4,104,768]{2,1,0:T(8,128)(2,1)} %copy-done.18, s32[2]{0:T(128)} %pad_add_fusion.turn_ref), custom_call_target="tpu_custom_call" | custom-call | bytes 3661832 | tf_op jit(solution)/shard_map/pallas_call | solution.py:494
  269.2 3.1 %collective-permute-start.52 = (f32[1,768]{1,0:T(1,128)S(1)}, f32[1,768]{1,0:T(1,128)S(1)}, u32[]{:S(2)}, u32[]{:S(2)}) collective-permute-start(f32[1,768]{1,0:T(1,128)S(1)} %add.142), channel_id=1, source_target_pairs={{0,2},{2,0},{1,3},{3,1},{4,6},{6,4},{5,7},{7,5},{8,10},{10,8},{9,1... | collective-permute-start | bytes 9224 | tf_op jit(solution)/shard_map/ppermute | solution.py:519
  (213 shorter events, 57.4 us)
Async XLA Ops:
  2.6 12.3 %collective-permute-start.2 = (bf16[256,768]{1,0:T(8,128)(2,1)}, bf16[256,768]{1,0:T(8,128)(2,1)S(1)}, u32[]{:S(2)}, u32[]{:S(2)}) collective-permute-start(bf16[256,768]{1,0:T(8,128)(2,1)} %shard_map.323.n0), channel_id=1, source_target_pairs={{0,2},{2,0},{1,3},{3,1},{4,6},{6,4},{5,7},{7,5},{8,10},{10,8},{9,1... | collective-permute-start | bytes 1179656 | tf_op jit(solution)/shard_map/ppermute | solution.py:519
  14.2 15.6 %collective-permute-start.4 = (bf16[384,768]{1,0:T(8,128)(2,1)S(1)}, bf16[384,768]{1,0:T(8,128)(2,1)}, u32[]{:S(2)}, u32[]{:S(2)}) collective-permute-start(bf16[384,768]{1,0:T(8,128)(2,1)S(1)} %pad_maximum_fusion.3.w0), channel_id=1, source_target_pairs={{0,2},{2,0},{1,3},{3,1},{4,6},{6,4},{5,7},{7,5},{8,10},{10,8},{9,1... | collective-permute-start | bytes 1769480 | tf_op jit(solution)/shard_map/ppermute | solution.py:519
  29.9 2.5 collective-permute-start.5
  29.9 3.2 %collective-permute-start.8 = (bf16[384,768]{1,0:T(8,128)(2,1)S(1)}, bf16[384,768]{1,0:T(8,128)(2,1)}, u32[]{:S(2)}, u32[]{:S(2)}) collective-permute-start(bf16[384,768]{1,0:T(8,128)(2,1)S(1)} %pad_maximum_fusion.3.w0), channel_id=1, source_target_pairs={{0,1},{1,0},{2,3},{3,2},{4,5},{5,4},{6,7},{7,6},{8,9},{9,8},{10,11... | collective-permute-start | bytes 1769480 | tf_op jit(solution)/shard_map/ppermute | solution.py:515
  30.4 3.2 %collective-permute-start.9 = (bf16[384,768]{1,0:T(8,128)(2,1)}, bf16[384,768]{1,0:T(8,128)(2,1)}, u32[]{:S(2)}, u32[]{:S(2)}) collective-permute-start(bf16[384,768]{1,0:T(8,128)(2,1)} %collective-permute-done.4.w2), channel_id=1, source_target_pairs={{0,1},{1,0},{2,3},{3,2},{4,5},{5,4},{6,7},{7,6},{8,9},{9,8},{10,11... | collective-permute-start | bytes 1769480 | tf_op jit(solution)/shard_map/ppermute | solution.py:515
  30.7 9.9 %collective-permute-start.7 = (bf16[192,768]{1,0:T(8,128)(2,1)S(1)}, bf16[192,768]{1,0:T(8,128)(2,1)S(1)}, u32[]{:S(2)}, u32[]{:S(2)}) collective-permute-start(bf16[192,768]{1,0:T(8,128)(2,1)S(1)} %fusion.7), channel_id=1, source_target_pairs={{0,2},{2,0},{1,3},{3,1},{4,6},{6,4},{5,7},{7,5},{8,10},{10,8},{9,1... | collective-permute-start | bytes 884744 | tf_op jit(solution)/shard_map/ppermute | solution.py:519
  32.4 16.2 %collective-permute-start.6 = (bf16[256,768]{1,0:T(8,128)(2,1)S(1)}, bf16[256,768]{1,0:T(8,128)(2,1)S(1)}, u32[]{:S(2)}, u32[]{:S(2)}) collective-permute-start(bf16[256,768]{1,0:T(8,128)(2,1)S(1)} %add_convert_fusion.4), channel_id=1, source_target_pairs={{0,2},{2,0},{1,3},{3,1},{4,6},{6,4},{5,7},{7,5},{8,10},{10,8},{9,1... | collective-permute-start | bytes 1179656 | tf_op jit(solution)/shard_map/ppermute | solution.py:519
  40.6 8.3 %collective-permute-start.11 = (bf16[192,768]{1,0:T(8,128)(2,1)S(1)}, bf16[192,768]{1,0:T(8,128)(2,1)S(1)}, u32[]{:S(2)}, u32[]{:S(2)}) collective-permute-start(bf16[192,768]{1,0:T(8,128)(2,1)S(1)} %collective-permute-done.7.w2), channel_id=1, source_target_pairs={{0,4},{4,0},{8,12},{12,8},{16,20},{20,16},{24,28},{28,24},{1,5},{5... | collective-permute-start | bytes 884744 | tf_op jit(solution)/shard_map/ppermute | solution.py:536
  42.1 8.2 %collective-permute-start.10 = (bf16[384,768]{1,0:T(8,128)(2,1)S(1)}, bf16[384,768]{1,0:T(8,128)(2,1)S(1)}, u32[]{:S(2)}, u32[]{:S(2)}) collective-permute-start(bf16[384,768]{1,0:T(8,128)(2,1)S(1)} %pad_maximum_fusion.w0), channel_id=1, source_target_pairs={{0,1},{1,0},{2,3},{3,2},{4,5},{5,4},{6,7},{7,6},{8,9},{9,8},{10,11... | collective-permute-start | bytes 1769480 | tf_op jit(solution)/shard_map/ppermute | solution.py:515
  42.2 8.1 %collective-permute-start.12 = (bf16[192,768]{1,0:T(8,128)(2,1)S(1)}, bf16[192,768]{1,0:T(8,128)(2,1)}, u32[]{:S(2)}, u32[]{:S(2)}) collective-permute-start(bf16[192,768]{1,0:T(8,128)(2,1)S(1)} %collective-permute-done.7.w2), channel_id=1, source_target_pairs={{0,1},{1,0},{2,3},{3,2},{4,5},{5,4},{6,7},{7,6},{8,9},{9,8},{10,11... | collective-permute-start | bytes 884744 | tf_op jit(solution)/shard_map/ppermute | solution.py:515
  48.9 13.7 %collective-permute-start.17 = (bf16[256,768]{1,0:T(8,128)(2,1)S(1)}, bf16[256,768]{1,0:T(8,128)(2,1)S(1)}, u32[]{:S(2)}, u32[]{:S(2)}) collective-permute-start(bf16[256,768]{1,0:T(8,128)(2,1)S(1)} %copy-done.27), channel_id=1, source_target_pairs={{0,2},{2,0},{1,3},{3,1},{4,6},{6,4},{5,7},{7,5},{8,10},{10,8},{9,1... | collective-permute-start | bytes 1179656 | tf_op jit(solution)/shard_map/ppermute | solution.py:519
  49.6 15.0 %collective-permute-start.16 = (bf16[256,768]{1,0:T(8,128)(2,1)S(1)}, bf16[256,768]{1,0:T(8,128)(2,1)S(1)}, u32[]{:S(2)}, u32[]{:S(2)}) collective-permute-start(bf16[256,768]{1,0:T(8,128)(2,1)S(1)} %copy-done.27), channel_id=1, source_target_pairs={{0,1},{1,0},{2,3},{3,2},{4,5},{5,4},{6,7},{7,6},{8,9},{9,8},{10,11... | collective-permute-start | bytes 1179656 | tf_op jit(solution)/shard_map/ppermute | solution.py:515
  62.6 2.0 collective-permute-start.18
  63.0 8.7 %collective-permute-start.14 = (bf16[256,768]{1,0:T(8,128)(2,1)}, bf16[256,768]{1,0:T(8,128)(2,1)S(1)}, u32[]{:S(2)}, u32[]{:S(2)}) collective-permute-start(bf16[256,768]{1,0:T(8,128)(2,1)} %get-tuple-element.134.g0), channel_id=1, source_target_pairs={{0,1},{1,0},{2,3},{3,2},{4,5},{5,4},{6,7},{7,6},{8,9},{9,8},{10,11... | collective-permute-start | bytes 1179656 | tf_op jit(solution)/shard_map/ppermute | solution.py:515
  63.2 14.9 %collective-permute-start.15 = (bf16[256,768]{1,0:T(8,128)(2,1)}, bf16[256,768]{1,0:T(8,128)(2,1)S(1)}, u32[]{:S(2)}, u32[]{:S(2)}) collective-permute-start(bf16[256,768]{1,0:T(8,128)(2,1)} %get-tuple-element.134.g0), channel_id=1, source_target_pairs={{0,2},{2,0},{1,3},{3,1},{4,6},{6,4},{5,7},{7,5},{8,10},{10,8},{9,1... | collective-permute-start | bytes 1179656 | tf_op jit(solution)/shard_map/ppermute | solution.py:519
  78.0 1.9 collective-permute-start.19
  91.2 12.5 %collective-permute-start.22 = (bf16[256,768]{1,0:T(8,128)(2,1)S(1)}, bf16[256,768]{1,0:T(8,128)(2,1)S(1)}, u32[]{:S(2)}, u32[]{:S(2)}) collective-permute-start(bf16[256,768]{1,0:T(8,128)(2,1)S(1)} %add_convert_fusion.3), channel_id=1, source_target_pairs={{0,2},{2,0},{1,3},{3,1},{4,6},{6,4},{5,7},{7,5},{8,10},{10,8},{9,1... | collective-permute-start | bytes 1179656 | tf_op jit(solution)/shard_map/ppermute | solution.py:519
  102.1 31.4 %collective-permute-start.25 = (bf16[4,192,768]{2,1,0:T(8,128)(2,1)}, bf16[4,192,768]{2,1,0:T(8,128)(2,1)S(1)}, u32[]{:S(2)}, u32[]{:S(2)}) collective-permute-start(bf16[4,192,768]{2,1,0:T(8,128)(2,1)} %get-tuple-element.149), channel_id=1, source_target_pairs={{0,4},{4,0},{8,12},{12,8},{16,20},{20,16},{24,28},{28,24},{1,5},{5... | collective-permute-start | bytes 3538952 | tf_op jit(solution)/shard_map/ppermute | solution.py:536
  122.5 11.0 %collective-permute-start.24 = (bf16[256,768]{1,0:T(8,128)(2,1)}, bf16[256,768]{1,0:T(8,128)(2,1)}, u32[]{:S(2)}, u32[]{:S(2)}) collective-permute-start(bf16[256,768]{1,0:T(8,128)(2,1)} %get-tuple-element.156.u0), channel_id=1, source_target_pairs={{0,2},{2,0},{1,3},{3,1},{4,6},{6,4},{5,7},{7,5},{8,10},{10,8},{9,1... | collective-permute-start | bytes 1179656 | tf_op jit(solution)/shard_map/ppermute | solution.py:519
  134.6 5.6 %collective-permute-start.26 = (bf16[2,8,104,768]{3,2,1,0:T(8,128)(2,1)}, bf16[2,8,104,768]{3,2,1,0:T(8,128)(2,1)S(1)}, u32[]{:S(2)}, u32[]{:S(2)}) collective-permute-start(bf16[2,8,104,768]{3,2,1,0:T(8,128)(2,1)} %get-tuple-element.167), channel_id=1, source_target_pairs={{0,1},{1,0},{2,3},{3,2},{4,5},{5,4},{6,7},{7,6},{8,9},{9,8},{10,11... | collective-permute-start | bytes 7667720 | tf_op jit(solution)/shard_map/ppermute | solution.py:515
  134.6 7.4 %collective-permute-start.23 = (bf16[256,768]{1,0:T(8,128)(2,1)S(1)}, bf16[256,768]{1,0:T(8,128)(2,1)S(1)}, u32[]{:S(2)}, u32[]{:S(2)}) collective-permute-start(bf16[256,768]{1,0:T(8,128)(2,1)S(1)} %copy-done.44), channel_id=1, source_target_pairs={{0,1},{1,0},{2,3},{3,2},{4,5},{5,4},{6,7},{7,6},{8,9},{9,8},{10,11... | collective-permute-start | bytes 1179656 | tf_op jit(solution)/shard_map/ppermute | solution.py:515
  135.1 7.6 %collective-permute-start.27 = (bf16[256,768]{1,0:T(8,128)(2,1)}, bf16[256,768]{1,0:T(8,128)(2,1)S(1)}, u32[]{:S(2)}, u32[]{:S(2)}) collective-permute-start(bf16[256,768]{1,0:T(8,128)(2,1)} %collective-permute-done.24.u2), channel_id=1, source_target_pairs={{0,1},{1,0},{2,3},{3,2},{4,5},{5,4},{6,7},{7,6},{8,9},{9,8},{10,11... | collective-permute-start | bytes 1179656 | tf_op jit(solution)/shard_map/ppermute | solution.py:515
  135.1 22.3 %collective-permute-start.28 = (bf16[2,192,768]{2,1,0:T(8,128)(2,1)}, bf16[2,192,768]{2,1,0:T(8,128)(2,1)}, u32[]{:S(2)}, u32[]{:S(2)}) collective-permute-start(bf16[2,192,768]{2,1,0:T(8,128)(2,1)} %get-tuple-element.222), channel_id=1, source_target_pairs={{0,8},{4,12},{8,0},{12,4},{16,24},{20,28},{24,16},{28,20},{1,9},{5... | collective-permute-start | bytes 1769480 | tf_op jit(solution)/shard_map/ppermute | solution.py:536
  140.5 30.2 %collective-permute-start.33 = (bf16[8,104,768]{2,1,0:T(8,128)(2,1)S(1)}, bf16[8,104,768]{2,1,0:T(8,128)(2,1)S(1)}, u32[]{:S(2)}, u32[]{:S(2)}) collective-permute-start(bf16[8,104,768]{2,1,0:T(8,128)(2,1)S(1)} %fusion.1), channel_id=1, source_target_pairs={{0,2},{2,0},{1,3},{3,1},{4,6},{6,4},{5,7},{7,5},{8,10},{10,8},{9,1... | collective-permute-start | bytes 3833864 | tf_op jit(solution)/shard_map/ppermute | solution.py:519
  159.3 3.1 %collective-permute-start.29 = (bf16[2,256,768]{2,1,0:T(8,128)(2,1)}, bf16[2,256,768]{2,1,0:T(8,128)(2,1)S(1)}, u32[]{:S(2)}, u32[]{:S(2)}) collective-permute-start(bf16[2,256,768]{2,1,0:T(8,128)(2,1)} %get-tuple-element.182), channel_id=1, source_target_pairs={{0,1},{1,0},{2,3},{3,2},{4,5},{5,4},{6,7},{7,6},{8,9},{9,8},{10,11... | collective-permute-start | bytes 2359304 | tf_op jit(solution)/shard_map/ppermute | solution.py:515
  159.3 19.9 %collective-permute-start.32 = (bf16[1,192,768]{2,1,0:T(8,128)(2,1)}, bf16[1,192,768]{2,1,0:T(8,128)(2,1)}, u32[]{:S(2)}, u32[]{:S(2)}) collective-permute-start(bf16[1,192,768]{2,1,0:T(8,128)(2,1)} %add_convert_fusion.11), channel_id=1, source_target_pairs={{0,16},{4,20},{8,24},{12,28},{16,0},{20,4},{24,8},{28,12},{1,17},{... | collective-permute-start | bytes 884744 | tf_op jit(solution)/shard_map/ppermute | solution.py:536
  161.9 18.6 %collective-permute-start.31 = (bf16[4,104,768]{2,1,0:T(8,128)(2,1)}, bf16[4,104,768]{2,1,0:T(8,128)(2,1)}, u32[]{:S(2)}, u32[]{:S(2)}) collective-permute-start(bf16[4,104,768]{2,1,0:T(8,128)(2,1)} %get-tuple-element.181), channel_id=1, source_target_pairs={{0,4},{4,0},{8,12},{12,8},{16,20},{20,16},{24,28},{28,24},{1,5},{5... | collective-permute-start | bytes 1916936 | tf_op jit(solution)/shard_map/ppermute | solution.py:536
  171.3 25.4 %collective-permute-start.36 = (bf16[4,104,768]{2,1,0:T(8,128)(2,1)S(1)}, bf16[4,104,768]{2,1,0:T(8,128)(2,1)S(1)}, u32[]{:S(2)}, u32[]{:S(2)}) collective-permute-start(bf16[4,104,768]{2,1,0:T(8,128)(2,1)S(1)} %slice.165), channel_id=1, source_target_pairs={{0,4},{4,0},{8,12},{12,8},{16,20},{20,16},{24,28},{28,24},{1,5},{5... | collective-permute-start | bytes 1916936 | tf_op jit(solution)/shard_map/ppermute | solution.py:536
  181.7 14.3 %collective-permute-start.34 = (bf16[2,104,768]{2,1,0:T(8,128)(2,1)S(1)}, bf16[2,104,768]{2,1,0:T(8,128)(2,1)S(1)}, u32[]{:S(2)}, u32[]{:S(2)}) collective-permute-start(bf16[2,104,768]{2,1,0:T(8,128)(2,1)S(1)} %get-tuple-element.225), channel_id=1, source_target_pairs={{0,8},{4,12},{8,0},{12,4},{16,24},{20,28},{24,16},{28,20},{1,9},{5... | collective-permute-start | bytes 958472 | tf_op jit(solution)/shard_map/ppermute | solution.py:536
  183.4 30.8 %collective-permute-start.30 = (bf16[256,768]{1,0:T(8,128)(2,1)S(1)}, bf16[256,768]{1,0:T(8,128)(2,1)S(1)}, u32[]{:S(2)}, u32[]{:S(2)}) collective-permute-start(bf16[256,768]{1,0:T(8,128)(2,1)S(1)} %copy-done.34), channel_id=1, source_target_pairs={{0,2},{2,0},{1,3},{3,1},{4,6},{6,4},{5,7},{7,5},{8,10},{10,8},{9,1... | collective-permute-start | bytes 1179656 | tf_op jit(solution)/shard_map/ppermute | solution.py:519
  184.7 18.7 %collective-permute-start.42 = (bf16[1,192,768]{2,1,0:T(8,128)(2,1)S(1)}, bf16[1,192,768]{2,1,0:T(8,128)(2,1)S(1)}, u32[]{:S(2)}, u32[]{:S(2)}) collective-permute-start(bf16[1,192,768]{2,1,0:T(8,128)(2,1)S(1)} %add_convert_fusion.9), channel_id=1, source_target_pairs={{0,16},{4,20},{8,24},{12,28},{16,0},{20,4},{24,8},{28,12},{1,17},{... | collective-permute-start | bytes 884744 | tf_op jit(solution)/shard_map/ppermute | solution.py:536
  196.0 10.4 %collective-permute-start.35 = (bf16[1,104,768]{2,1,0:T(8,128)(2,1)S(1)}, bf16[1,104,768]{2,1,0:T(8,128)(2,1)S(1)}, u32[]{:S(2)}, u32[]{:S(2)}) collective-permute-start(bf16[1,104,768]{2,1,0:T(8,128)(2,1)S(1)} %add_convert_fusion.16), channel_id=1, source_target_pairs={{0,16},{4,20},{8,24},{12,28},{16,0},{20,4},{24,8},{28,12},{1,17},{... | collective-permute-start | bytes 479240 | tf_op jit(solution)/shard_map/ppermute | solution.py:536
  196.8 12.3 %collective-permute-start.37 = (bf16[2,104,768]{2,1,0:T(8,128)(2,1)S(1)}, bf16[2,104,768]{2,1,0:T(8,128)(2,1)S(1)}, u32[]{:S(2)}, u32[]{:S(2)}) collective-permute-start(bf16[2,104,768]{2,1,0:T(8,128)(2,1)S(1)} %get-tuple-element.224), channel_id=1, source_target_pairs={{0,8},{4,12},{8,0},{12,4},{16,24},{20,28},{24,16},{28,20},{1,9},{5... | collective-permute-start | bytes 958472 | tf_op jit(solution)/shard_map/ppermute | solution.py:536
  206.5 13.0 %collective-permute-start.40 = (bf16[1,104,768]{2,1,0:T(8,128)(2,1)S(1)}, bf16[1,104,768]{2,1,0:T(8,128)(2,1)S(1)}, u32[]{:S(2)}, u32[]{:S(2)}) collective-permute-start(bf16[1,104,768]{2,1,0:T(8,128)(2,1)S(1)} %add_convert_fusion.15), channel_id=1, source_target_pairs={{0,16},{4,20},{8,24},{12,28},{16,0},{20,4},{24,8},{28,12},{1,17},{... | collective-permute-start | bytes 479240 | tf_op jit(solution)/shard_map/ppermute | solution.py:536
  209.1 13.6 %collective-permute-start.44 = (bf16[1,104,768]{2,1,0:T(8,128)(2,1)S(1)}, bf16[1,104,768]{2,1,0:T(8,128)(2,1)S(1)}, u32[]{:S(2)}, u32[]{:S(2)}) collective-permute-start(bf16[1,104,768]{2,1,0:T(8,128)(2,1)S(1)} %add_convert_fusion.14), channel_id=1, source_target_pairs={{0,16},{4,20},{8,24},{12,28},{16,0},{20,4},{24,8},{28,12},{1,17},{... | collective-permute-start | bytes 479240 | tf_op jit(solution)/shard_map/ppermute | solution.py:536
  210.5 14.9 %collective-permute-start.45 = (bf16[2,96,768]{2,1,0:T(8,128)(2,1)S(1)}, bf16[2,96,768]{2,1,0:T(8,128)(2,1)S(1)}, u32[]{:S(2)}, u32[]{:S(2)}) collective-permute-start(bf16[2,96,768]{2,1,0:T(8,128)(2,1)S(1)} %get-tuple-element.227), channel_id=1, source_target_pairs={{0,8},{4,12},{8,0},{12,4},{16,24},{20,28},{24,16},{28,20},{1,9},{5... | collective-permute-start | bytes 884744 | tf_op jit(solution)/shard_map/ppermute | solution.py:536
  212.6 12.9 %collective-permute-start.43 = (bf16[2,96,768]{2,1,0:T(8,128)(2,1)S(1)}, bf16[2,96,768]{2,1,0:T(8,128)(2,1)S(1)}, u32[]{:S(2)}, u32[]{:S(2)}) collective-permute-start(bf16[2,96,768]{2,1,0:T(8,128)(2,1)S(1)} %get-tuple-element.228), channel_id=1, source_target_pairs={{0,4},{4,0},{8,12},{12,8},{16,20},{20,16},{24,28},{28,24},{1,5},{5... | collective-permute-start | bytes 884744 | tf_op jit(solution)/shard_map/ppermute | solution.py:536
  219.5 14.8 %collective-permute-start.41 = (bf16[2,104,768]{2,1,0:T(8,128)(2,1)S(1)}, bf16[2,104,768]{2,1,0:T(8,128)(2,1)S(1)}, u32[]{:S(2)}, u32[]{:S(2)}) collective-permute-start(bf16[2,104,768]{2,1,0:T(8,128)(2,1)S(1)} %pad_maximum_fusion.6), channel_id=1, source_target_pairs={{0,8},{4,12},{8,0},{12,4},{16,24},{20,28},{24,16},{28,20},{1,9},{5... | collective-permute-start | bytes 958472 | tf_op jit(solution)/shard_map/ppermute | solution.py:536
  219.6 27.1 %collective-permute-start.38 = (bf16[2,256,768]{2,1,0:T(8,128)(2,1)S(1)}, bf16[2,256,768]{2,1,0:T(8,128)(2,1)S(1)}, u32[]{:S(2)}, u32[]{:S(2)}) collective-permute-start(bf16[2,256,768]{2,1,0:T(8,128)(2,1)S(1)} %copy-done.40), channel_id=1, source_target_pairs={{0,1},{1,0},{2,3},{3,2},{4,5},{5,4},{6,7},{7,6},{8,9},{9,8},{10,11... | collective-permute-start | bytes 2359304 | tf_op jit(solution)/shard_map/ppermute | solution.py:515
  222.7 11.7 %collective-permute-start.47 = (bf16[1,104,768]{2,1,0:T(8,128)(2,1)S(1)}, bf16[1,104,768]{2,1,0:T(8,128)(2,1)S(1)}, u32[]{:S(2)}, u32[]{:S(2)}) collective-permute-start(bf16[1,104,768]{2,1,0:T(8,128)(2,1)S(1)} %add_convert_fusion.12), channel_id=1, source_target_pairs={{0,16},{4,20},{8,24},{12,28},{16,0},{20,4},{24,8},{28,12},{1,17},{... | collective-permute-start | bytes 479240 | tf_op jit(solution)/shard_map/ppermute | solution.py:536
  225.5 14.7 %collective-permute-start.49 = (bf16[4,96,768]{2,1,0:T(8,128)(2,1)S(1)}, bf16[4,96,768]{2,1,0:T(8,128)(2,1)S(1)}, u32[]{:S(2)}, u32[]{:S(2)}) collective-permute-start(bf16[4,96,768]{2,1,0:T(8,128)(2,1)S(1)} %pad_maximum_fusion.5.low_ref), channel_id=1, source_target_pairs={{0,4},{4,0},{8,12},{12,8},{16,20},{20,16},{24,28},{28,24},{1,5},{5... | collective-permute-start | bytes 1769480 | tf_op jit(solution)/shard_map/ppermute | solution.py:536
  234.5 10.5 %collective-permute-start.48 = (bf16[2,104,768]{2,1,0:T(8,128)(2,1)S(1)}, bf16[2,104,768]{2,1,0:T(8,128)(2,1)S(1)}, u32[]{:S(2)}, u32[]{:S(2)}) collective-permute-start(bf16[2,104,768]{2,1,0:T(8,128)(2,1)S(1)} %pad_maximum_fusion.7), channel_id=1, source_target_pairs={{0,8},{4,12},{8,0},{12,4},{16,24},{20,28},{24,16},{28,20},{1,9},{5... | collective-permute-start | bytes 958472 | tf_op jit(solution)/shard_map/ppermute | solution.py:536
  234.6 24.2 %collective-permute-start.46 = (bf16[4,104,768]{2,1,0:T(8,128)(2,1)S(1)}, bf16[4,104,768]{2,1,0:T(8,128)(2,1)S(1)}, u32[]{:S(2)}, u32[]{:S(2)}) collective-permute-start(bf16[4,104,768]{2,1,0:T(8,128)(2,1)S(1)} %pad_maximum_fusion.1.low_ref), channel_id=1, source_target_pairs={{0,4},{4,0},{8,12},{12,8},{16,20},{20,16},{24,28},{28,24},{1,5},{5... | collective-permute-start | bytes 1916936 | tf_op jit(solution)/shard_map/ppermute | solution.py:536
  236.2 18.9 %collective-permute-start.53 = (bf16[4,96,768]{2,1,0:T(8,128)(2,1)S(1)}, bf16[4,96,768]{2,1,0:T(8,128)(2,1)S(1)}, u32[]{:S(2)}, u32[]{:S(2)}) collective-permute-start(bf16[4,96,768]{2,1,0:T(8,128)(2,1)S(1)} %pad_maximum_fusion.4.low_ref), channel_id=1, source_target_pairs={{0,8},{4,12},{8,0},{12,4},{16,24},{20,28},{24,16},{28,20},{1,9},{5... | collective-permute-start | bytes 1769480 | tf_op jit(solution)/shard_map/ppermute | solution.py:536
  245.1 20.3 %collective-permute-start.50 = (bf16[4,104,768]{2,1,0:T(8,128)(2,1)S(1)}, bf16[4,104,768]{2,1,0:T(8,128)(2,1)S(1)}, u32[]{:S(2)}, u32[]{:S(2)}) collective-permute-start(bf16[4,104,768]{2,1,0:T(8,128)(2,1)S(1)} %pad_maximum_fusion.2.low_ref), channel_id=1, source_target_pairs={{0,4},{4,0},{8,12},{12,8},{16,20},{20,16},{24,28},{28,24},{1,5},{5... | collective-permute-start | bytes 1916936 | tf_op jit(solution)/shard_map/ppermute | solution.py:536
  246.8 18.6 %collective-permute-start.39 = (bf16[256,768]{1,0:T(8,128)(2,1)S(1)}, bf16[256,768]{1,0:T(8,128)(2,1)S(1)}, u32[]{:S(2)}, u32[]{:S(2)}) collective-permute-start(bf16[256,768]{1,0:T(8,128)(2,1)S(1)} %fusion.2), channel_id=1, source_target_pairs={{0,2},{2,0},{1,3},{3,1},{4,6},{6,4},{5,7},{7,5},{8,10},{10,8},{9,1... | collective-permute-start | bytes 1179656 | tf_op jit(solution)/shard_map/ppermute | solution.py:519
  265.4 3.9 %collective-permute-start.51 = (f32[1,768]{1,0:T(1,128)S(1)}, f32[1,768]{1,0:T(1,128)S(1)}, u32[]{:S(2)}, u32[]{:S(2)}) collective-permute-start(f32[1,768]{1,0:T(1,128)S(1)} %slice.155), channel_id=1, source_target_pairs={{0,1},{1,0},{2,3},{3,2},{4,5},{5,4},{6,7},{7,6},{8,9},{9,8},{10,11... | collective-permute-start | bytes 9224 | tf_op jit(solution)/shard_map/ppermute | solution.py:515
  269.2 4.7 %collective-permute-start.52 = (f32[1,768]{1,0:T(1,128)S(1)}, f32[1,768]{1,0:T(1,128)S(1)}, u32[]{:S(2)}, u32[]{:S(2)}) collective-permute-start(f32[1,768]{1,0:T(1,128)S(1)} %add.142), channel_id=1, source_target_pairs={{0,2},{2,0},{1,3},{3,1},{4,6},{6,4},{5,7},{7,5},{8,10},{10,8},{9,1... | collective-permute-start | bytes 9224 | tf_op jit(solution)/shard_map/ppermute | solution.py:519
  (55 other events, 321.0 us)
